TPU v7x, 32 devices: a 4x4x1 block of a 4x4x8 slice. The times are simulated.
32 devices in a mesh: dp: 1 (over z), kv: 32 (over y, x, core).
Axes of the slice: x: 4, y: 4, z: 1, core: 2. Of those that a mesh axis runs over, the one named last changes fastest.
The devices are a block of a 4x4x8 slice.
Arguments:
- x_first: bfloat16 [16, 4096], P('dp')
- next_emb: bfloat16 [2, 16, 4096], P(None, 'dp')
- k_cache: bfloat16 [16, 8192, 8, 128], P('dp', 'kv')
- v_cache: bfloat16 [16, 8192, 8, 128], P('dp', 'kv')
- seq_len: int32 [16], P('dp')
- ln1_gain: float32 [4096], replicated
- ln1_bias: float32 [4096], replicated
- w_q: bfloat16 [4096, 4096], replicated
- b_q: float32 [4096], replicated
- w_k: bfloat16 [4096, 1024], replicated
- b_k: float32 [1024], replicated
- w_v: bfloat16 [4096, 1024], replicated
- b_v: float32 [1024], replicated
- w_o: bfloat16 [4096, 4096], replicated
- b_o: float32 [4096], replicated
- ln2_gain: float32 [4096], replicated
- ln2_bias: float32 [4096], replicated
- w_router: bfloat16 [4096, 16], replicated
- w_gate: bfloat16 [16, 4096, 960], P(None, None, 'kv')
- w_up: bfloat16 [16, 4096, 960], P(None, None, 'kv')
- w_down: bfloat16 [16, 960, 4096], P(None, 'kv')
- long_factor: float32 [64], replicated
- expert_idx: int32 [3, 16, 2], P(None, 'dp')
- route_mask: int32 [3, 16, 2, 16], P(None, 'dp')
Outputs:
- output 1: bfloat16 [3, 16, 4096], P(None, 'dp')
- output 2: bfloat16 [16, 3, 8, 128], P('dp')
- output 3: bfloat16 [16, 3, 8, 128], P('dp')
All inputs are finite; a program needn't handle non-finite values.
Results may differ from a plain program's by a relative error of at most 0.0117903.
Values sent between devices are 32-bit elements.
A program may use at most 768 MiB of HBM per device.

v0:
```python
import math
import jax
import jax.numpy as jnp
from jax import lax
from jax.sharding import PartitionSpec as P

ROPE_BASE = 10000.0
ROPE_MSCALE = math.sqrt(1.0 + math.log(32.0) / math.log(4096.0))
NORM_EPS = 1e-5
NEG_FILL = -1e30


def layer_norm(x_in, gain_vec, bias_vec):
    x_f32 = x_in.astype(jnp.float32)
    mean_val = jnp.mean(x_f32, axis=-1, keepdims=True)
    centered = x_f32 - mean_val
    var_val = jnp.mean(centered * centered, axis=-1, keepdims=True)
    return (centered * lax.rsqrt(var_val + NORM_EPS) * gain_vec + bias_vec).astype(jnp.bfloat16)


def rotate_heads(x_in, angles):
    half_dim = x_in.shape[-1] // 2
    cos_half = jnp.cos(angles) * ROPE_MSCALE
    sin_half = jnp.sin(angles) * ROPE_MSCALE
    cos_full = jnp.concatenate([cos_half, cos_half], axis=-1)[:, None, :]
    sin_full = jnp.concatenate([sin_half, sin_half], axis=-1)[:, None, :]
    x_f32 = x_in.astype(jnp.float32)
    rotated = jnp.concatenate([-x_f32[..., half_dim:], x_f32[..., :half_dim]], axis=-1)
    return (x_f32 * cos_full + rotated * sin_full).astype(jnp.bfloat16)


def inverse_freq(long_factor, head_dim):
    half_dim = head_dim // 2
    return 1.0 / (long_factor * ROPE_BASE ** (jnp.arange(half_dim, dtype=jnp.float32) * 2.0 / head_dim))


def partial_stats(q_grp, keys, values, keep_mask):
    scores = jnp.einsum('bkgd,btkd->bkgt', q_grp, keys, preferred_element_type=jnp.float32) * (q_grp.shape[-1] ** -0.5)
    keep_full = keep_mask[:, None, None, :]
    scores = jnp.where(keep_full, scores, NEG_FILL)
    run_max = jnp.max(scores, axis=-1)
    weights = jnp.where(keep_full, jnp.exp(scores - run_max[..., None]), 0.0)
    run_sum = jnp.sum(weights, axis=-1)
    out_part = jnp.einsum('bkgt,btkd->bkgd', weights.astype(jnp.bfloat16), values, preferred_element_type=jnp.float32)
    return run_max, run_sum, out_part


def combine_stats(max_all, sum_all, out_all):
    top_max = jnp.max(max_all, axis=0, keepdims=True)
    factor = jnp.exp(max_all - top_max)
    total_sum = jnp.sum(sum_all * factor, axis=0)
    merged = jnp.sum(out_all * factor[..., None], axis=0)
    return merged / total_sum[..., None]


def gate_matrix(h_moe, w_router, idx_step, mask_step):
    logits = jnp.dot(h_moe, w_router, preferred_element_type=jnp.float32)
    masked = jnp.where(mask_step == 1, logits[:, None, :], NEG_FILL)
    gate_probs = jax.nn.softmax(masked, axis=-1)
    chosen = idx_step[..., None] == jnp.arange(logits.shape[-1])[None, None, :]
    return jnp.sum(jnp.where(chosen, gate_probs, 0.0), axis=1)


def expert_part(h_moe, gate_mat, w_gate, w_up, w_down):
    act_gate = jnp.einsum('bd,edf->bef', h_moe, w_gate, preferred_element_type=jnp.float32)
    act_up = jnp.einsum('bd,edf->bef', h_moe, w_up, preferred_element_type=jnp.float32)
    mixed_act = (gate_mat[:, :, None] * jax.nn.silu(act_gate) * act_up).astype(jnp.bfloat16)
    return jnp.einsum('bef,efd->bd', mixed_act, w_down, preferred_element_type=jnp.float32).astype(jnp.bfloat16)


def solution(mesh):
    def layer_steps(x_first, next_emb, k_cache, v_cache, seq_len, ln1_gain, ln1_bias, w_q, b_q, w_k, b_k, w_v, b_v, w_o, b_o, ln2_gain, ln2_bias, w_router, w_gate, w_up, w_down, long_factor, expert_idx, route_mask):
        batch_rows, shard_len, kv_heads, head_dim = k_cache.shape
        q_heads = w_q.shape[1] // head_dim
        q_group = q_heads // kv_heads
        shard_id = lax.axis_index('kv')
        positions = shard_id * shard_len + jnp.arange(shard_len)
        cache_keep = positions[None, :] < seq_len[:, None]
        inv_freq = inverse_freq(long_factor, head_dim)
        step_inputs = [x_first] + [next_emb[emb_idx] for emb_idx in range(next_emb.shape[0])]
        new_keys = []
        new_values = []
        hidden = []
        for step_idx, x_in in enumerate(step_inputs):
            h_norm = layer_norm(x_in, ln1_gain, ln1_bias)
            q_new = (jnp.dot(h_norm, w_q, preferred_element_type=jnp.float32) + b_q).astype(jnp.bfloat16).reshape(batch_rows, q_heads, head_dim)
            k_new = (jnp.dot(h_norm, w_k, preferred_element_type=jnp.float32) + b_k).astype(jnp.bfloat16).reshape(batch_rows, kv_heads, head_dim)
            v_new = (jnp.dot(h_norm, w_v, preferred_element_type=jnp.float32) + b_v).astype(jnp.bfloat16).reshape(batch_rows, kv_heads, head_dim)
            angles = (seq_len + step_idx).astype(jnp.float32)[:, None] * inv_freq[None, :]
            q_grp = rotate_heads(q_new, angles).reshape(batch_rows, kv_heads, q_group, head_dim)
            new_keys.append(rotate_heads(k_new, angles))
            new_values.append(v_new)
            tail_k = jnp.stack(new_keys, axis=1)
            tail_v = jnp.stack(new_values, axis=1)
            run_max, run_sum, out_part = partial_stats(q_grp, k_cache, v_cache, cache_keep)
            packed = jnp.concatenate([run_max[..., None], run_sum[..., None], out_part], axis=-1)
            gathered = lax.all_gather(packed, 'kv')
            tail_keep = jnp.ones((batch_rows, step_idx + 1), jnp.bool_)
            tail_max, tail_sum, tail_out = partial_stats(q_grp, tail_k, tail_v, tail_keep)
            max_all = jnp.concatenate([gathered[..., 0], tail_max[None]], axis=0)
            sum_all = jnp.concatenate([gathered[..., 1], tail_sum[None]], axis=0)
            out_all = jnp.concatenate([gathered[..., 2:], tail_out[None]], axis=0)
            attn_out = combine_stats(max_all, sum_all, out_all).reshape(batch_rows, q_heads * head_dim).astype(jnp.bfloat16)
            x_mid = (x_in.astype(jnp.float32) + jnp.dot(attn_out, w_o, preferred_element_type=jnp.float32) + b_o).astype(jnp.bfloat16)
            h_moe = layer_norm(x_mid, ln2_gain, ln2_bias)
            gate_mat = gate_matrix(h_moe, w_router, expert_idx[step_idx], route_mask[step_idx])
            moe_part = expert_part(h_moe, gate_mat, w_gate, w_up, w_down)
            moe_sum = lax.psum(moe_part.astype(jnp.float32), 'kv')
            hidden.append((x_mid.astype(jnp.float32) + moe_sum).astype(jnp.bfloat16))
        return jnp.stack(hidden, axis=0), tail_k, tail_v

    replicated = P()
    in_specs = (P('dp'), P(None, 'dp'), P('dp', 'kv'), P('dp', 'kv'), P('dp')) + (replicated,) * 13 + (P(None, None, 'kv'), P(None, None, 'kv'), P(None, 'kv'), replicated, P(None, 'dp'), P(None, 'dp'))
    out_specs = (P(None, 'dp'), P('dp'), P('dp'))
    return jax.shard_map(layer_steps, mesh=mesh, in_specs=in_specs, out_specs=out_specs, check_vma=False)
```

profile of v0, /device:TPU:97, one launch (start us, length us, event | category | flops | bytes accessed | tf_op | source)
XLA Modules:
  0.0 556.4 jit_solution(16048306486351748814)
XLA Ops:
  8.7 1.1 convert_reduce_fusion.2
  9.8 1.2 fusion.145
  11.1 15.0 %fusion.31 = f32[16,4096]{1,0:T(8,128)S(1)} fusion(bf16[4096,4096]{1,0:T(8,128)(2,1)} %param.31, f32[4096]{0:T(1024)} %param.32, f32[16]{0:T(128)S(1)} %add_rsqrt_fusion.3, f32[16]{0:T(128)S(1)} %get-tuple-element.109, f32[4096]{0:T(1024)} %param.30, f32[4096]{0:T(1024)} %param.29, bf16[2,16,4096]{2,1,0:T(8,128)(2,1)} %param.25), kind=kOutput, calls=%fused_computation.43 | convolution fusion | flops 537460736 | bytes 33996928 | tf_op jit(solution)/shard_map/dot_general | solution.py:86
  26.7 12.9 %fusion.37 = f32[16,4096]{1,0:T(8,128)S(1)} fusion(bf16[4096,4096]{1,0:T(8,128)(2,1)} %param.31, f32[4096]{0:T(1024)S(1)} %copy-done.7, f32[16]{0:T(128)S(1)} %add_rsqrt_fusion.1, f32[16]{0:T(128)S(1)} %get-tuple-element.108, f32[4096]{0:T(1024)S(1)} %copy-done.4, f32[4096]{0:T(1024)S(1)} %copy-done.5, bf16[2,16,4096]{2,1,0:T(8,128)(2,1)S(1)} %copy-done.2), kind=kOutput, calls=%fused_computation.49 | convolution fusion | flops 537460736 | bytes 33997824 | tf_op jit(solution)/shard_map/dot_general | solution.py:86
  40.5 5.8 %fusion.280 = (f32[16,8,4]{2,1,0:T(8,128)S(1)}, f32[16,8,4,256]{3,2,1,0:T(4,128)S(1)}) fusion(bf16[16,8,4,128]{3,2,1,0:T(4,128)(2,1)S(1)} %fusion.157, bf16[16,256,8,128]{3,2,1,0:T(8,128)(2,1)} %param.26, pred[16,256]{1,0:T(8,128)(4,1)S(1)} %broadcast_compare_fusion), kind=kOutput, calls=%fused_computation.347 | convolution fusion | flops 33947136 | bytes 9050112 | tf_op jit(solution)/shard_map/bkgd,btkd->bkgt/dot_general | solution.py:38
  46.6 5.7 %fusion.278 = (f32[16,8,4]{2,1,0:T(8,128)S(1)}, f32[16,8,4,256]{3,2,1,0:T(4,128)S(1)}) fusion(bf16[16,8,4,128]{3,2,1,0:T(4,128)(2,1)S(1)} %fusion.161, bf16[16,256,8,128]{3,2,1,0:T(8,128)(2,1)} %param.26, pred[16,256]{1,0:T(8,128)(4,1)S(1)} %broadcast_compare_fusion), kind=kOutput, calls=%fused_computation.345 | convolution fusion | flops 33947136 | bytes 9050112 | tf_op jit(solution)/shard_map/bkgd,btkd->bkgt/dot_general | solution.py:38
  52.8 13.3 %fusion.25 = f32[16,4096]{1,0:T(8,128)S(1)} fusion(bf16[4096,4096]{1,0:T(8,128)(2,1)} %param.31, f32[4096]{0:T(1024)S(1)} %copy-done.7, bf16[16,4096]{1,0:T(8,128)(2,1)S(1)} %copy-done.3, f32[4096]{0:T(1024)S(1)} %copy-done.4, f32[4096]{0:T(1024)S(1)} %copy-done.5, f32[16]{0:T(128)S(1)} %add_rsqrt_fusion.5, f32[16]{0:T(128)S(1)} %broadcast_multiply_fusion.5), kind=kOutput, calls=%fused_computation.37 | convolution fusion | flops 537460736 | bytes 33996928 | tf_op jit(solution)/shard_map/dot_general | solution.py:86
  66.8 5.7 %fusion.279 = (f32[16,8,4]{2,1,0:T(8,128)S(1)}, f32[16,8,4,256]{3,2,1,0:T(4,128)S(1)}) fusion(bf16[16,8,4,128]{3,2,1,0:T(4,128)(2,1)S(1)} %fusion.153, bf16[16,256,8,128]{3,2,1,0:T(8,128)(2,1)} %param.26, pred[16,256]{1,0:T(8,128)(4,1)S(1)} %broadcast_compare_fusion), kind=kOutput, calls=%fused_computation.346 | convolution fusion | flops 33947136 | bytes 9050112 | tf_op jit(solution)/shard_map/bkgd,btkd->bkgt/dot_general | solution.py:38
  72.5 1.2 fusion.124
  73.7 0.9 copy.592
  74.6 4.6 fusion.11
  79.2 0.9 copy.591
  80.8 0.9 copy.593
  81.8 0.9 copy.622
  82.7 0.9 copy.621
  83.6 4.6 fusion.9
  88.8 0.9 copy.623
  89.9 0.9 copy.572
  90.8 0.9 copy.571
  91.7 4.6 fusion.13
  96.9 0.9 copy.573
  98.2 4.6 fusion.90
  102.8 4.6 fusion.86
  109.5 0.9 copy.602
  110.4 4.6 fusion.91
  115.1 4.6 fusion.87
  120.2 4.6 fusion.94
  126.6 0.9 copy.633
  127.5 4.6 fusion.95
  133.7 19.7 %all-gather.9.cloned.1.call-done = f32[512,8,4,130]{3,1,2,0:T(8,128)} async-done(((f32[16,8,4,130]{3,1,2,0:T(8,128)}), f32[512,8,4,130]{3,1,2,0:T(8,128)}) %all-gather.9.cloned.1.call-update) | async-done | bytes 8519696 | tf_op jit(solution)/shard_map/all_gather | solution.py:97
  153.4 11.6 %slice.125 = f32[32,16,8,4,128]{4,2,3,1,0:T(8,128)} slice(f32[32,16,8,4,130]{4,2,3,1,0:T(8,128)} %bitcast.234), slice={[0:32], [0:16], [0:8], [0:4], [2:130]} | slice | bytes 16777216 | tf_op jit(solution)/shard_map/slice | solution.py:102
  165.0 57.2 %all-gather.11.cloned.1.call-done = f32[512,8,4,130]{3,1,2,0:T(8,128)} async-done(((f32[16,8,4,130]{3,1,2,0:T(8,128)}), f32[512,8,4,130]{3,1,2,0:T(8,128)}) %all-gather.11.cloned.1.call-update) | async-done | bytes 8519696 | tf_op jit(solution)/shard_map/all_gather | solution.py:97
  222.2 11.2 %slice.132 = f32[32,16,8,4,128]{4,2,3,1,0:T(8,128)} slice(f32[32,16,8,4,130]{4,2,3,1,0:T(8,128)} %bitcast.236), slice={[0:32], [0:16], [0:8], [0:4], [2:130]} | slice | bytes 16777216 | tf_op jit(solution)/shard_map/slice | solution.py:102
  233.4 13.6 %fusion.274 = (f32[32,16,8,4,1]{4,2,3,1,0:T(8,128)}, f32[16,8,4]{1,2,0:T(4,128)S(1)}, f32[32,16,8,4,1]{4,2,3,1,0:T(8,128)}) fusion(f32[32,16,8,4,130]{4,2,3,1,0:T(8,128)} %bitcast.235), kind=kLoop, calls=%fused_computation.341 | loop fusion | flops 15872 | bytes 264192 | tf_op jit(solution)/shard_map/slice | solution.py:100
  247.0 2.8 copy-done.1
  249.8 7.5 %fusion.275 = (f32[32,16,8,4,1]{4,2,3,1,0:T(8,128)}, f32[16,8,4]{1,2,0:T(4,128)S(1)}, f32[32,16,8,4,1]{4,2,3,1,0:T(8,128)}) fusion(f32[32,16,8,4,130]{4,2,3,1,0:T(8,128)S(1)} %bitcast.237), kind=kLoop, calls=%fused_computation.342 | loop fusion | flops 15872 | bytes 264192 | tf_op jit(solution)/shard_map/slice | solution.py:100
  257.3 33.7 %all-gather.7.cloned.1.call-done = f32[512,8,4,130]{3,1,2,0:T(8,128)} async-done(((f32[16,8,4,130]{3,1,2,0:T(8,128)}), f32[512,8,4,130]{3,1,2,0:T(8,128)}) %all-gather.7.cloned.1.call-update) | async-done | bytes 8519696 | tf_op jit(solution)/shard_map/all_gather | solution.py:97
  291.0 11.1 %fusion.273 = (f32[32,16,8,4,1]{4,2,3,1,0:T(8,128)}, f32[16,8,4]{1,2,0:T(4,128)S(1)}, f32[32,16,8,4,1]{4,2,3,1,0:T(8,128)}) fusion(f32[32,16,8,4,130]{4,2,3,1,0:T(8,128)} %bitcast.238), kind=kLoop, calls=%fused_computation.340 | loop fusion | flops 15872 | bytes 264192 | tf_op jit(solution)/shard_map/slice | solution.py:100
  302.1 11.2 %slice.118 = f32[32,16,8,4,128]{4,2,3,1,0:T(8,128)} slice(f32[32,16,8,4,130]{4,2,3,1,0:T(8,128)} %bitcast.239), slice={[0:32], [0:16], [0:8], [0:4], [2:130]} | slice | bytes 16777216 | tf_op jit(solution)/shard_map/slice | solution.py:102
  313.4 6.4 %copy.600 = f32[32,16,8,4,1]{0,2,4,3,1:T(8,128)S(1)} copy(f32[32,16,8,4,1]{4,2,3,1,0:T(8,128)} %get-tuple-element.49) | data formatting | bytes 131072 | tf_op jit(solution)/shard_map/slice | solution.py:100
  319.8 6.4 %copy.608 = f32[32,16,8,4,1]{0,2,4,3,1:T(8,128)S(1)} copy(f32[32,16,8,4,1]{4,2,3,1,0:T(8,128)} %get-tuple-element.51) | data formatting | bytes 131072 | tf_op jit(solution)/shard_map/slice | solution.py:101
  326.5 1.2 copy.607
  327.7 5.3 fusion.7
  333.3 13.1 %fusion.283 = (f32[16]{0:T(128)S(1)}, f32[16,4096]{1,0:T(8,128)S(1)}) fusion(f32[4096]{0:T(1024)S(1)} %copy-done.6, bf16[16,4096]{1,0:T(8,128)(2,1)S(1)} %convert_element_type.350, bf16[4096,4096]{1,0:T(8,128)(2,1)} %param.37, bf16[2,16,4096]{2,1,0:T(8,128)(2,1)S(1)} %copy-done.2), kind=kOutput, calls=%fused_computation.350 | convolution fusion | flops 537264128 | bytes 34095168 | tf_op jit(solution)/shard_map/dot_general | solution.py:104
  346.9 6.4 %copy.631 = f32[32,16,8,4,1]{0,2,4,3,1:T(8,128)S(1)} copy(f32[32,16,8,4,1]{4,2,3,1,0:T(8,128)} %get-tuple-element.52) | data formatting | bytes 131072 | tf_op jit(solution)/shard_map/slice | solution.py:100
  353.3 6.4 %copy.639 = f32[32,16,8,4,1]{0,2,4,3,1:T(8,128)S(1)} copy(f32[32,16,8,4,1]{4,2,3,1,0:T(8,128)} %get-tuple-element.54) | data formatting | bytes 131072 | tf_op jit(solution)/shard_map/slice | solution.py:101
  360.0 1.2 copy.638
  361.2 5.3 fusion.8
  366.8 12.9 %fusion.284 = (f32[16]{0:T(128)S(1)}, f32[16,4096]{1,0:T(8,128)S(1)}) fusion(f32[4096]{0:T(1024)S(1)} %copy-done.6, bf16[16,4096]{1,0:T(8,128)(2,1)S(1)} %convert_element_type.378, bf16[4096,4096]{1,0:T(8,128)(2,1)} %param.37, bf16[2,16,4096]{2,1,0:T(8,128)(2,1)S(1)} %copy-done.2), kind=kOutput, calls=%fused_computation.351 | convolution fusion | flops 537264128 | bytes 34095168 | tf_op jit(solution)/shard_map/dot_general | solution.py:104
  380.9 6.4 %copy.579 = f32[32,16,8,4,1]{0,2,4,3,1:T(8,128)S(1)} copy(f32[32,16,8,4,1]{4,2,3,1,0:T(8,128)} %get-tuple-element.48) | data formatting | bytes 131072 | tf_op jit(solution)/shard_map/slice | solution.py:101
  387.3 6.4 %copy.574 = f32[32,16,8,4,1]{0,2,4,3,1:T(8,128)S(1)} copy(f32[32,16,8,4,1]{4,2,3,1,0:T(8,128)} %get-tuple-element.46) | data formatting | bytes 131072 | tf_op jit(solution)/shard_map/slice | solution.py:100
  394.1 1.2 copy.578
  395.4 5.3 fusion.6
  401.0 13.5 %fusion.281 = (f32[16]{0:T(128)S(1)}, f32[16,4096]{1,0:T(8,128)S(1)}) fusion(f32[4096]{0:T(1024)S(1)} %copy-done.6, bf16[16,4096]{1,0:T(8,128)(2,1)S(1)} %convert_element_type.319, bf16[4096,4096]{1,0:T(8,128)(2,1)} %param.37, bf16[16,4096]{1,0:T(8,128)(2,1)S(1)} %copy-done.3), kind=kOutput, calls=%fused_computation.348 | convolution fusion | flops 537264128 | bytes 34095168 | tf_op jit(solution)/shard_map/dot_general | solution.py:104
  415.0 2.8 fusion.55
  418.0 2.9 fusion.53
  421.1 2.9 fusion.51
  425.2 9.1 %fusion.29 = f32[16,4096]{1,0:T(8,128)} fusion(bf16[16,30,4096]{2,0,1:T(8,128)(2,1)} %param.44, bf16[16,4096,30]{1,0,2:T(8,128)(2,1)} %param.43, bf16[16,4096]{1,0:T(8,128)(2,1)S(1)} %get-tuple-element.69, f32[16,16,30]{2,0,1:T(8,128)S(1)} %fusion.55, f32[16,16]{0,1:T(8,128)S(1)} %copy.583), kind=kOutput, calls=%fused_computation.41 | convolution fusion | flops 126013952 | bytes 8289280 | tf_op jit(solution)/shard_map/bef,efd->bd/dot_general | solution.py:68
  434.2 8.9 %fusion.35 = f32[16,4096]{1,0:T(8,128)} fusion(bf16[16,30,4096]{2,0,1:T(8,128)(2,1)} %param.44, bf16[16,4096,30]{1,0,2:T(8,128)(2,1)} %param.43, bf16[16,4096]{1,0:T(8,128)(2,1)S(1)} %get-tuple-element.70, f32[16,16,30]{2,0,1:T(8,128)S(1)} %fusion.53, f32[16,16]{0,1:T(8,128)S(1)} %copy.613), kind=kOutput, calls=%fused_computation.47 | convolution fusion | flops 126013952 | bytes 8289280 | tf_op jit(solution)/shard_map/bef,efd->bd/dot_general | solution.py:68
  443.1 8.9 %fusion.41 = f32[16,4096]{1,0:T(8,128)} fusion(bf16[16,30,4096]{2,0,1:T(8,128)(2,1)} %param.44, bf16[16,4096,30]{1,0,2:T(8,128)(2,1)} %param.43, bf16[16,4096]{1,0:T(8,128)(2,1)S(1)} %get-tuple-element.71, f32[16,16,30]{2,0,1:T(8,128)S(1)} %fusion.51, f32[16,16]{0,1:T(8,128)S(1)} %copy.644), kind=kOutput, calls=%fused_computation.53 | convolution fusion | flops 126013952 | bytes 8289280 | tf_op jit(solution)/shard_map/bef,efd->bd/dot_general | solution.py:68
  452.7 93.3 %all-reduce.3.cloned.1.call-done = (f32[16,4096]{1,0:T(8,128)}, f32[16,4096]{1,0:T(8,128)}, f32[16,4096]{1,0:T(8,128)}) async-done(((f32[16,4096]{1,0:T(8,128)}, f32[16,4096]{1,0:T(8,128)}, f32[16,4096]{1,0:T(8,128)}), (f32[16,4096]{1,0:T(8,128)}, f32[16,4096]{1,0:T(8,128)}, f32[16,4096]{1,0:T(8,128)})) %all-reduce.3.cloned.1.call-update) | async-done | bytes 786448 | tf_op jit(solution)/shard_map/psum | solution.py:108
  546.0 1.0 fusion.176
  546.9 1.0 fusion.177
  547.9 1.0 fusion.178
  (182 shorter events, 19.7 us)
Async XLA Ops:
  7.2 410.7 %copy-start = (bf16[4096,16]{0,1:T(8,128)(2,1)S(1)}, bf16[4096,16]{0,1:T(8,128)(2,1)}, u32[]{:S(2)}) copy-start(bf16[4096,16]{0,1:T(8,128)(2,1)} %param.41) | copy-start | bytes 393220
  7.2 146.2 %all-gather.9.cloned.1.call-start = ((), (), s32[]{:S(2)}) async-start(), calls=%async_computation.1 | async-start | bytes 17301504 | tf_op jit(solution)/shard_map/all_gather | solution.py:97
  9.8 16.3 %copy-start.15 = (f32[16]{0:T(128)}, f32[16]{0:T(128)S(1)}, u32[]{:S(2)}) copy-start(f32[16]{0:T(128)S(1)} %get-tuple-element.109) | copy-start | bytes 196
  9.8 16.8 %copy-start.13 = (f32[16]{0:T(128)}, f32[16]{0:T(128)S(1)}, u32[]{:S(2)}) copy-start(f32[16]{0:T(128)S(1)} %get-tuple-element.108) | copy-start | bytes 196
  11.0 15.1 %copy-start.25 = (f32[16]{0:T(128)}, f32[16]{0:T(128)S(1)}, u32[]{:S(2)}) copy-start(f32[16]{0:T(128)S(1)} %add_rsqrt_fusion.3) | copy-start | bytes 196
  11.0 15.5 %copy-start.30 = (s32[16]{0:T(128)S(1)}, s32[16]{0:T(128)}, u32[]{:S(2)}) copy-start(s32[16]{0:T(128)} %param.28) | copy-start | bytes 196
  11.1 15.6 %copy-start.2 = (bf16[2,16,4096]{2,1,0:T(8,128)(2,1)S(1)}, bf16[2,16,4096]{2,1,0:T(8,128)(2,1)}, u32[]{:S(2)}) copy-start(bf16[2,16,4096]{2,1,0:T(8,128)(2,1)} %param.25) | copy-start | bytes 786436
  11.1 15.6 %copy-start.4 = (f32[4096]{0:T(1024)S(1)}, f32[4096]{0:T(1024)}, u32[]{:S(2)}) copy-start(f32[4096]{0:T(1024)} %param.30) | copy-start | bytes 49156
  11.1 15.6 %copy-start.5 = (f32[4096]{0:T(1024)S(1)}, f32[4096]{0:T(1024)}, u32[]{:S(2)}) copy-start(f32[4096]{0:T(1024)} %param.29) | copy-start | bytes 49156
  11.1 15.6 %copy-start.7 = (f32[4096]{0:T(1024)S(1)}, f32[4096]{0:T(1024)}, u32[]{:S(2)}) copy-start(f32[4096]{0:T(1024)} %param.32) | copy-start | bytes 49156
  26.6 45.9 %copy-start.19 = (pred[16,256]{1,0:T(8,128)(4,1)}, pred[16,256]{1,0:T(8,128)(4,1)S(1)}, u32[]{:S(2)}) copy-start(pred[16,256]{1,0:T(8,128)(4,1)S(1)} %broadcast_compare_fusion) | copy-start | bytes 12292
  26.7 12.9 %copy-start.23 = (f32[16]{0:T(128)}, f32[16]{0:T(128)S(1)}, u32[]{:S(2)}) copy-start(f32[16]{0:T(128)S(1)} %add_rsqrt_fusion.1) | copy-start | bytes 196
  40.5 11.8 %copy-start.8 = (bf16[16,8,4,128]{3,2,1,0:T(4,128)(2,1)}, bf16[16,8,4,128]{3,2,1,0:T(4,128)(2,1)S(1)}, u32[]{:S(2)}) copy-start(bf16[16,8,4,128]{3,2,1,0:T(4,128)(2,1)S(1)} %fusion.157) | copy-start | bytes 393220
  40.5 11.8 %copy-start.3 = (bf16[16,4096]{1,0:T(8,128)(2,1)S(1)}, bf16[16,4096]{1,0:T(8,128)(2,1)}, u32[]{:S(2)}) copy-start(bf16[16,4096]{1,0:T(8,128)(2,1)} %param.24) | copy-start | bytes 393220
  52.5 13.6 %copy-start.21 = (f32[16]{0:T(128)}, f32[16]{0:T(128)S(1)}, u32[]{:S(2)}) copy-start(f32[16]{0:T(128)S(1)} %broadcast_multiply_fusion.5) | copy-start | bytes 196
  52.7 13.3 %copy-start.27 = (f32[16]{0:T(128)}, f32[16]{0:T(128)S(1)}, u32[]{:S(2)}) copy-start(f32[16]{0:T(128)S(1)} %add_rsqrt_fusion.5) | copy-start | bytes 196
  80.1 11.5 %copy-start.20 = (pred[16,256]{1,0:T(8,128)(4,1)S(1)}, pred[16,256]{1,0:T(8,128)(4,1)}, u32[]{:S(2)}) copy-start(pred[16,256]{1,0:T(8,128)(4,1)} %copy-done.19) | copy-start | bytes 12292
  81.7 140.5 %all-gather.11.cloned.1.call-start = ((), (), s32[]{:S(2)}) async-start(), calls=%async_computation.2 | async-start | bytes 17301504 | tf_op jit(solution)/shard_map/all_gather | solution.py:97
  88.2 9.9 %copy-start.11 = (f32[1024]{0:T(1024)S(1)}, f32[1024]{0:T(1024)}, u32[]{:S(2)}) copy-start(f32[1024]{0:T(1024)} %param.34) | copy-start | bytes 12292
  88.2 9.9 %copy-start.16 = (f32[16]{0:T(128)S(1)}, f32[16]{0:T(128)}, u32[]{:S(2)}) copy-start(f32[16]{0:T(128)} %copy-done.15) | copy-start | bytes 196
  88.2 9.9 %copy-start.26 = (f32[16]{0:T(128)S(1)}, f32[16]{0:T(128)}, u32[]{:S(2)}) copy-start(f32[16]{0:T(128)} %copy-done.25) | copy-start | bytes 196
  89.8 201.2 %all-gather.7.cloned.1.call-start = ((), (), s32[]{:S(2)}) async-start(), calls=%async_computation | async-start | bytes 17301504 | tf_op jit(solution)/shard_map/all_gather | solution.py:97
  91.7 11.2 %copy-start.22 = (f32[16]{0:T(128)S(1)}, f32[16]{0:T(128)}, u32[]{:S(2)}) copy-start(f32[16]{0:T(128)} %copy-done.21) | copy-start | bytes 196
  91.7 11.2 %copy-start.28 = (f32[16]{0:T(128)S(1)}, f32[16]{0:T(128)}, u32[]{:S(2)}) copy-start(f32[16]{0:T(128)} %copy-done.27) | copy-start | bytes 196
  97.9 10.0 %copy-start.9 = (bf16[16,8,4,128]{3,2,1,0:T(4,128)(2,1)S(1)}, bf16[16,8,4,128]{3,2,1,0:T(4,128)(2,1)}, u32[]{:S(2)}) copy-start(bf16[16,8,4,128]{3,2,1,0:T(4,128)(2,1)} %copy-done.8) | copy-start | bytes 393220
  97.9 12.5 %copy-start.12 = (f32[1024]{0:T(1024)S(1)}, f32[1024]{0:T(1024)}, u32[]{:S(2)}) copy-start(f32[1024]{0:T(1024)} %param.36) | copy-start | bytes 12292
  97.9 448.1 %all-reduce.3.cloned.1.call-start = ((), (), s32[]{:S(2)}) async-start(), calls=%async_computation.3 | async-start | bytes 1572864 | tf_op jit(solution)/shard_map/psum | solution.py:108
  110.4 9.8 %copy-start.14 = (f32[16]{0:T(128)S(1)}, f32[16]{0:T(128)}, u32[]{:S(2)}) copy-start(f32[16]{0:T(128)} %copy-done.13) | copy-start | bytes 196
  110.4 9.8 %copy-start.24 = (f32[16]{0:T(128)S(1)}, f32[16]{0:T(128)}, u32[]{:S(2)}) copy-start(f32[16]{0:T(128)} %copy-done.23) | copy-start | bytes 196
  124.8 8.6 %copy-start.29 = (s32[3,16,2]{1,2,0:T(2,128)S(1)}, s32[3,16,2]{1,2,0:T(2,128)}, u32[]{:S(2)}) copy-start(s32[3,16,2]{1,2,0:T(2,128)} %param.46) | copy-start | bytes 1156
  125.0 40.0 %copy-start.10 = (bf16[16,3,8,128]{3,2,1,0:T(8,128)(2,1)}, bf16[16,3,8,128]{3,2,1,0:T(8,128)(2,1)S(1)}, u32[]{:S(2)}) copy-start(bf16[16,3,8,128]{3,2,1,0:T(8,128)(2,1)S(1)} %pad_maximum_fusion.5) | copy-start | bytes 294916
  233.4 16.4 %copy-start.1 = (f32[512,8,4,130]{3,1,2,0:T(8,128)S(1)}, f32[512,8,4,130]{3,1,2,0:T(8,128)}, u32[]{:S(2)}) copy-start(f32[512,8,4,130]{3,1,2,0:T(8,128)} %all-gather.11.cloned.1.call-done) | copy-start | bytes 25559044
  326.1 7.2 %copy-start.6 = (f32[4096]{0:T(1024)S(1)}, f32[4096]{0:T(1024)}, u32[]{:S(2)}) copy-start(f32[4096]{0:T(1024)} %param.38) | copy-start | bytes 49156
  401.0 13.8 %copy-start.17 = (f32[4096]{0:T(1024)S(1)}, f32[4096]{0:T(1024)}, u32[]{:S(2)}) copy-start(f32[4096]{0:T(1024)} %param.40) | copy-start | bytes 49156
  401.0 13.8 %copy-start.18 = (f32[4096]{0:T(1024)S(1)}, f32[4096]{0:T(1024)}, u32[]{:S(2)}) copy-start(f32[4096]{0:T(1024)} %param.39) | copy-start | bytes 49156
  401.0 14.0 %copy-start.31 = (bf16[16,4096,30]{1,0,2:T(8,128)(2,1)S(1)}, bf16[16,4096,30]{1,0,2:T(8,128)(2,1)}, u32[]{:S(2)}) copy-start(bf16[16,4096,30]{1,0,2:T(8,128)(2,1)} %param.42) | copy-start | bytes 11796484
  414.8 9.3 %copy-start.32 = (s32[3,16,2,16]{3,2,1,0:T(2,128)S(1)}, s32[3,16,2,16]{3,2,1,0:T(2,128)}, u32[]{:S(2)}) copy-start(s32[3,16,2,16]{3,2,1,0:T(2,128)} %param.47) | copy-start | bytes 18436
Sparse Core Ops, SparseCore 0:
  81.8 71.5 all-gather.8
  155.5 66.6 all-gather.10
  224.3 66.6 all-gather.6
  452.2 93.7 all-reduce.2
where the time goes:
time: 566 us; the launch traced here: 556 us
  waiting for transfers between devices  204 us (36%)
  matrix products  177 us (31%)
  local copies, waits for them, and re-layouts  94.3 us (17%)
  other arithmetic  65.4 us (12%)
  between operations  14.9 us (3%)
    all_gather x3, waiting for transfers between devices, layer_steps(): gathered = lax.all_gather(packed, 'kv')  111 us
    psum x1, waiting for transfers between devices, layer_steps(): moe_sum = lax.psum(moe_part.astype(jnp.float32), 'kv')  93.3 us
    dot_general x3, matrix products, layer_steps(): jnp.dot(h_norm, w_q, preferred_element_type=jnp.float32) + b_q  41.2 us
    dot_general x3, matrix products, layer_steps(): jnp.dot(attn_out, w_o, preferred_element_type=jnp.float32)  39.6 us
    slice x3, local copies, waits for them, and re-layouts, layer_steps(): out_all = jnp.concatenate([gathered[..., 2:], tail_out[None]], axis=0)  34 us
    slice x3, other arithmetic, layer_steps(): max_all = jnp.concatenate([gathered[..., 0], tail_max[None]], axis=0)  32.2 us
    dot_general x3, matrix products, expert_part(): jnp.einsum('bef,efd->bd', mixed_act, w_down, preferred_element_type=jnp.f...  26.8 us
    slice x3, local copies, waits for them, and re-layouts, layer_steps(): max_all = jnp.concatenate([gathered[..., 0], tail_max[None]], axis=0)  19.1 us
  transfers between devices with their start and end apart: 4, of which 4 were waited for; matrix products, arithmetic and copies ran while one was open for 17% of the time, Pallas kernels for 0%

commit v1 on v0

--- a/solution.py
+++ b/solution.py
@@ -36,7 +36,7 @@
 
 def partial_stats(q_grp, keys, values, keep_mask):
     scores = jnp.einsum('bkgd,btkd->bkgt', q_grp, keys, preferred_element_type=jnp.float32) * (q_grp.shape[-1] ** -0.5)
-    keep_full = keep_mask[:, None, None, :]
+    keep_full = keep_mask
     scores = jnp.where(keep_full, scores, NEG_FILL)
     run_max = jnp.max(scores, axis=-1)
     weights = jnp.where(keep_full, jnp.exp(scores - run_max[..., None]), 0.0)
@@ -77,37 +77,37 @@
         positions = shard_id * shard_len + jnp.arange(shard_len)
         cache_keep = positions[None, :] < seq_len[:, None]
         inv_freq = inverse_freq(long_factor, head_dim)
-        step_inputs = [x_first] + [next_emb[emb_idx] for emb_idx in range(next_emb.shape[0])]
-        new_keys = []
-        new_values = []
-        hidden = []
-        for step_idx, x_in in enumerate(step_inputs):
-            h_norm = layer_norm(x_in, ln1_gain, ln1_bias)
-            q_new = (jnp.dot(h_norm, w_q, preferred_element_type=jnp.float32) + b_q).astype(jnp.bfloat16).reshape(batch_rows, q_heads, head_dim)
-            k_new = (jnp.dot(h_norm, w_k, preferred_element_type=jnp.float32) + b_k).astype(jnp.bfloat16).reshape(batch_rows, kv_heads, head_dim)
-            v_new = (jnp.dot(h_norm, w_v, preferred_element_type=jnp.float32) + b_v).astype(jnp.bfloat16).reshape(batch_rows, kv_heads, head_dim)
-            angles = (seq_len + step_idx).astype(jnp.float32)[:, None] * inv_freq[None, :]
-            q_grp = rotate_heads(q_new, angles).reshape(batch_rows, kv_heads, q_group, head_dim)
-            new_keys.append(rotate_heads(k_new, angles))
-            new_values.append(v_new)
-            tail_k = jnp.stack(new_keys, axis=1)
-            tail_v = jnp.stack(new_values, axis=1)
-            run_max, run_sum, out_part = partial_stats(q_grp, k_cache, v_cache, cache_keep)
-            packed = jnp.concatenate([run_max[..., None], run_sum[..., None], out_part], axis=-1)
-            gathered = lax.all_gather(packed, 'kv')
-            tail_keep = jnp.ones((batch_rows, step_idx + 1), jnp.bool_)
-            tail_max, tail_sum, tail_out = partial_stats(q_grp, tail_k, tail_v, tail_keep)
-            max_all = jnp.concatenate([gathered[..., 0], tail_max[None]], axis=0)
-            sum_all = jnp.concatenate([gathered[..., 1], tail_sum[None]], axis=0)
-            out_all = jnp.concatenate([gathered[..., 2:], tail_out[None]], axis=0)
-            attn_out = combine_stats(max_all, sum_all, out_all).reshape(batch_rows, q_heads * head_dim).astype(jnp.bfloat16)
-            x_mid = (x_in.astype(jnp.float32) + jnp.dot(attn_out, w_o, preferred_element_type=jnp.float32) + b_o).astype(jnp.bfloat16)
-            h_moe = layer_norm(x_mid, ln2_gain, ln2_bias)
-            gate_mat = gate_matrix(h_moe, w_router, expert_idx[step_idx], route_mask[step_idx])
-            moe_part = expert_part(h_moe, gate_mat, w_gate, w_up, w_down)
-            moe_sum = lax.psum(moe_part.astype(jnp.float32), 'kv')
-            hidden.append((x_mid.astype(jnp.float32) + moe_sum).astype(jnp.bfloat16))
-        return jnp.stack(hidden, axis=0), tail_k, tail_v
+        num_steps = next_emb.shape[0] + 1
+        x_all = jnp.concatenate([x_first[None], next_emb], axis=0)
+        rows = num_steps * batch_rows
+        h_norm = layer_norm(x_all, ln1_gain, ln1_bias).reshape(rows, -1)
+        q_new = (jnp.dot(h_norm, w_q, preferred_element_type=jnp.float32) + b_q).astype(jnp.bfloat16).reshape(rows, q_heads, head_dim)
+        k_new = (jnp.dot(h_norm, w_k, preferred_element_type=jnp.float32) + b_k).astype(jnp.bfloat16).reshape(rows, kv_heads, head_dim)
+        v_new = (jnp.dot(h_norm, w_v, preferred_element_type=jnp.float32) + b_v).astype(jnp.bfloat16).reshape(num_steps, batch_rows, kv_heads, head_dim)
+        steps = jnp.arange(num_steps)
+        angles = ((seq_len[None, :] + steps[:, None]).astype(jnp.float32)[:, :, None] * inv_freq).reshape(rows, -1)
+        q_rot = rotate_heads(q_new, angles).reshape(num_steps, batch_rows, kv_heads, q_group, head_dim)
+        q_grp = q_rot.transpose(1, 2, 0, 3, 4).reshape(batch_rows, kv_heads, num_steps * q_group, head_dim)
+        tail_k = rotate_heads(k_new, angles).reshape(num_steps, batch_rows, kv_heads, head_dim).transpose(1, 0, 2, 3)
+        tail_v = v_new.transpose(1, 0, 2, 3)
+        run_max, run_sum, out_part = partial_stats(q_grp, k_cache, v_cache, cache_keep[:, None, None, :])
+        packed = jnp.concatenate([run_max[..., None], run_sum[..., None], out_part], axis=-1)
+        gathered = lax.all_gather(packed, 'kv')
+        tail_keep = jnp.repeat(steps[None, :] <= steps[:, None], q_group, axis=0)[None, None]
+        tail_max, tail_sum, tail_out = partial_stats(q_grp, tail_k, tail_v, tail_keep)
+        max_all = jnp.concatenate([gathered[..., 0], tail_max[None]], axis=0)
+        sum_all = jnp.concatenate([gathered[..., 1], tail_sum[None]], axis=0)
+        out_all = jnp.concatenate([gathered[..., 2:], tail_out[None]], axis=0)
+        attn = combine_stats(max_all, sum_all, out_all).astype(jnp.bfloat16)
+        attn = attn.reshape(batch_rows, kv_heads, num_steps, q_group, head_dim).transpose(2, 0, 1, 3, 4).reshape(rows, q_heads * head_dim)
+        x_flat = x_all.reshape(rows, -1)
+        x_mid = (x_flat.astype(jnp.float32) + jnp.dot(attn, w_o, preferred_element_type=jnp.float32) + b_o).astype(jnp.bfloat16)
+        h_moe = layer_norm(x_mid, ln2_gain, ln2_bias)
+        gate_mat = gate_matrix(h_moe, w_router, expert_idx.reshape(rows, -1), route_mask.reshape(rows, *route_mask.shape[2:]))
+        moe_part = expert_part(h_moe, gate_mat, w_gate, w_up, w_down)
+        moe_sum = lax.psum(moe_part.astype(jnp.float32), 'kv')
+        hidden = (x_mid.astype(jnp.float32) + moe_sum).astype(jnp.bfloat16)
+        return hidden.reshape(num_steps, batch_rows, -1), tail_k, tail_v
 
     replicated = P()
     in_specs = (P('dp'), P(None, 'dp'), P('dp', 'kv'), P('dp', 'kv'), P('dp')) + (replicated,) * 13 + (P(None, None, 'kv'), P(None, None, 'kv'), P(None, 'kv'), replicated, P(None, 'dp'), P(None, 'dp'))

time: 566 us -> 450 us (0.80); the launches traced: 556 us -> 447 us
  matrix products: 177 us -> 61.6 us
  waiting for transfers between devices: 204 us -> 232 us
  local copies, waits for them, and re-layouts: 94.3 us -> 77.6 us
    all_gather x3 -> x1, waiting for transfers between devices: 111 us -> 140 us  [layer_steps(): gathered = lax.all_gather(packed, 'kv')]
    dot_general x3 -> x1, matrix products: 41.2 us -> 13.8 us  [layer_steps(): jnp.dot(h_norm, w_q, preferred_element_type=jnp.float32) + b_q]
    dot_general x6 -> x1, matrix products: 40.1 us -> 14.1 us  [layer_steps(): jnp.dot(attn, w_o, preferred_element_type=jnp.float32)]
    dot_general x3 -> x1, matrix products: 26.8 us -> 8.64 us  [expert_part(): jnp.einsum('bef,efd->bd', mixed_act, w_down, preferred_element_type=jnp.f...]
    dot_general x6 -> x2, matrix products: 18.2 us -> 6.15 us  [partial_stats(): jnp.einsum('bkgd,btkd->bkgt', q_grp, keys, preferred_element_type=jnp.flo...]
    slice x3 -> x1, local copies, waits for them, and re-layouts: 34 us -> 24.6 us  [layer_steps(): out_all = jnp.concatenate([gathered[..., 2:], tail_out[None]], axis=0)]
    dot_general x3 -> x1, matrix products: 13.8 us -> 4.95 us  [layer_steps(): jnp.dot(h_norm, w_k, preferred_element_type=jnp.float32) + b_k]
    dot_general x3 -> x1, matrix products: 13.9 us -> 5 us  [layer_steps(): jnp.dot(h_norm, w_v, preferred_element_type=jnp.float32) + b_v]
  transfers between devices with their start and end apart: 4 -> 2, of which waited for: 4 -> 2; matrix products, arithmetic and copies ran while one was open for 17% -> 4% of each run, Pallas kernels for 0% -> 0%
where the time goes in v1:
time: 450 us; the launch traced here: 447 us
  waiting for transfers between devices  232 us (52%)
  local copies, waits for them, and re-layouts  77.6 us (17%)
  matrix products  61.6 us (14%)
  other arithmetic  60.3 us (13%)
  between operations  15 us (3%)
    all_gather x1, waiting for transfers between devices, layer_steps(): gathered = lax.all_gather(packed, 'kv')  140 us
    psum x1, waiting for transfers between devices, layer_steps(): moe_sum = lax.psum(moe_part.astype(jnp.float32), 'kv')  92.2 us
    slice x1, other arithmetic, layer_steps(): max_all = jnp.concatenate([gathered[..., 0], tail_max[None]], axis=0)  33.6 us
    slice x1, local copies, waits for them, and re-layouts, layer_steps(): out_all = jnp.concatenate([gathered[..., 2:], tail_out[None]], axis=0)  24.6 us
    slice x1, local copies, waits for them, and re-layouts, layer_steps(): max_all = jnp.concatenate([gathered[..., 0], tail_max[None]], axis=0)  17.3 us
    slice x1, local copies, waits for them, and re-layouts, layer_steps(): sum_all = jnp.concatenate([gathered[..., 1], tail_sum[None]], axis=0)  17.3 us
    dot_general x1, matrix products, layer_steps(): jnp.dot(attn, w_o, preferred_element_type=jnp.float32)  14.1 us
    dot_general x1, matrix products, layer_steps(): jnp.dot(h_norm, w_q, preferred_element_type=jnp.float32) + b_q  13.8 us
  transfers between devices with their start and end apart: 2, of which 2 were waited for; matrix products, arithmetic and copies ran while one was open for 4% of the time, Pallas kernels for 0%

profile of v1, /device:TPU:97, one launch (start us, length us, event | category | flops | bytes accessed | tf_op | source)
XLA Modules:
  0.0 446.7 jit_solution(8243871198945358082)
XLA Ops:
  7.3 1.1 convert_reduce_fusion
  8.4 1.2 multiply_reduce_fusion.1
  9.6 0.1 div.51
  9.7 0.1 rsqrt.20
  9.8 1.2 fusion.51
  11.1 13.8 %fusion.11 = f32[48,4096]{1,0:T(8,128)S(1)} fusion(bf16[48,4096]{1,0:T(8,128)(2,1)S(1)} %fusion.51, bf16[4096,4096]{1,0:T(8,128)(2,1)} %param.31, f32[4096]{0:T(1024)} %param.32), kind=kOutput, calls=%fused_computation.15 | convolution fusion | flops 1611202560 | bytes 34750464 | tf_op jit(solution)/shard_map/dot_general | solution.py:84
  24.9 0.5 reshape.240
  25.4 0.1 copy.262
  25.6 0.3 fusion.96
  25.9 0.5 copy_negate_fusion
  26.4 0.5 copy.261
  26.9 0.2 fusion.81
  27.1 0.1 pad_maximum_fusion.2
  27.2 0.6 fusion.56
  27.8 0.3 copy.210
  28.1 5.7 %fusion.19 = (f32[16,8,12]{2,1,0:T(8,128)S(1)}, f32[16,8,12,256]{3,2,1,0:T(8,128)S(1)}) fusion(pred[16,256]{1,0:T(8,128)(4,1)S(1)} %broadcast_compare_fusion, bf16[16,256,8,128]{3,2,1,0:T(8,128)(2,1)} %param.26, bf16[16,8,12,128]{3,1,2,0:T(8,128)(2,1)S(1)} %bitcast.102), kind=kOutput, calls=%fused_computation.26 | convolution fusion | flops 101841408 | bytes 10364928 | tf_op jit(solution)/shard_map/bkgd,btkd->bkgt/dot_general | solution.py:38
  33.9 1.1 fusion.21
  34.9 1.9 copy.217
  36.9 5.8 %fusion.3 = f32[16,8,12,128]{3,2,1,0:T(8,128)} fusion(bf16[16,256,8,128]{3,2,1,0:T(8,128)(2,1)} %param.27, f32[16,8,12,256]{3,2,1,0:T(8,128)S(1)} %get-tuple-element.35, f32[16,8,12]{2,1,0:T(8,128)S(1)} %get-tuple-element.34, pred[16,256]{1,0:T(8,128)(4,1)S(1)} %broadcast_compare_fusion), kind=kOutput, calls=%fused_computation.4 | convolution fusion | flops 102629376 | bytes 10758144 | tf_op jit(solution)/shard_map/bkgt,btkd->bkgd/dot_general | solution.py:44
  42.6 0.9 copy.216
  43.5 2.7 pad_maximum_fusion
  46.2 2.4 copy.218
  48.7 0.3 all-reduce.2.cloned.1.call-start
  49.0 5.0 %fusion.31 = f32[6,8,8,128]{3,1,2,0:T(8,128)S(1)} fusion(bf16[48,4096]{1,0:T(8,128)(2,1)S(1)} %fusion.51, bf16[4096,1024]{1,0:T(8,128)(2,1)} %param.33, f32[1024]{0:T(1024)S(1)} %copy-done.11), kind=kOutput, calls=%fused_computation.38 | convolution fusion | flops 402800640 | bytes 8982528 | tf_op jit(solution)/shard_map/dot_general | solution.py:85
  54.0 0.1 broadcast_in_dim.122
  54.1 0.1 broadcast_in_dim.123
  54.2 0.1 slice_negate_fusion
  54.3 0.1 fusion.79
  54.4 0.4 fusion.97
  54.8 0.1 copy.229
  55.0 0.2 fusion.69
  55.2 0.9 copy.236
  56.1 1.8 copy.226
  57.9 5.0 %fusion.33 = bf16[6,8,8,128]{3,1,2,0:T(8,128)(2,1)S(1)} fusion(bf16[48,4096]{1,0:T(8,128)(2,1)S(1)} %fusion.51, bf16[4096,1024]{1,0:T(8,128)(2,1)} %param.35, f32[1024]{0:T(1024)S(1)} %copy-done.12), kind=kOutput, calls=%fused_computation.40 | convolution fusion | flops 402751488 | bytes 8884224 | tf_op jit(solution)/shard_map/dot_general | solution.py:86
  63.0 0.4 convolution_bitcast_fusion.1
  63.3 1.2 copy.223
  64.5 0.1 copy.240
  64.6 1.0 fusion.93
  65.6 139.7 %all-gather.3.cloned.1.call-done = f32[512,8,12,130]{3,1,2,0:T(8,128)} async-done(((f32[16,8,12,130]{3,1,2,0:T(8,128)}), f32[512,8,12,130]{3,1,2,0:T(8,128)}) %all-gather.3.cloned.1.call-update) | async-done | bytes 25559056 | tf_op jit(solution)/shard_map/all_gather | solution.py:95
  205.3 33.6 %fusion.95 = (f32[32,16,8,12,1]{4,2,3,1,0:T(8,128)}, f32[16,8,12]{1,2,0:T(8,128)S(1)}, f32[32,16,8,12,1]{4,2,3,1,0:T(8,128)}) fusion(f32[32,16,8,12,130]{4,2,3,1,0:T(8,128)} %bitcast.90), kind=kLoop, calls=%fused_computation.130 | loop fusion | flops 47616 | bytes 792576 | tf_op jit(solution)/shard_map/slice | solution.py:98
  238.9 24.6 %slice.30 = f32[32,16,8,12,128]{4,2,3,1,0:T(8,128)} slice(f32[32,16,8,12,130]{4,2,3,1,0:T(8,128)} %bitcast.91), slice={[0:32], [0:16], [0:8], [0:12], [2:130]} | slice | bytes 50331648 | tf_op jit(solution)/shard_map/slice | solution.py:100
  263.5 0.1 copy.228
  263.6 0.1 copy.230
  263.7 17.3 %copy.224 = f32[32,16,8,12,1]{0,2,4,3,1:T(8,128)S(1)} copy(f32[32,16,8,12,1]{4,2,3,1,0:T(8,128)} %get-tuple-element.23) | data formatting | bytes 393216 | tf_op jit(solution)/shard_map/slice | solution.py:98
  281.0 17.3 %copy.234 = f32[32,16,8,12,1]{0,2,4,3,1:T(8,128)S(1)} copy(f32[32,16,8,12,1]{4,2,3,1,0:T(8,128)} %get-tuple-element.25) | data formatting | bytes 393216 | tf_op jit(solution)/shard_map/slice | solution.py:99
  298.2 2.7 fusion.47
  301.0 4.8 %copy.231 = f32[33,16,8,12]{2,3,1,0:T(8,128)} copy(f32[33,16,8,12]{0,2,3,1:T(8,128)S(1)} %get-tuple-element.22) | data formatting | bytes 405504 | tf_op jit(solution)/shard_map/exp | solution.py:50
  305.7 0.1 copy.237
  305.8 0.1 copy.238
  306.0 10.3 %fusion.2 = f32[16,8,12,128]{3,1,2,0:T(8,128)S(1)} fusion(f32[1,16,8,12,128]{4,2,3,1,0:T(8,128)S(1)} %copy-done.2, f32[32,16,8,12,128]{4,2,3,1,0:T(8,128)} %slice.30, f32[33,16,8,12]{2,3,1,0:T(8,128)} %copy.231), kind=kLoop, calls=%fused_computation.3 | loop fusion | flops 19267584 | bytes 26941440 | tf_op jit(solution)/shard_map/reduce_sum | solution.py:52
  316.2 0.3 fusion.60
  316.5 0.2 copy.239
  316.7 0.3 reshape.237
  317.0 14.1 %fusion.98 = (f32[48]{0:T(128)S(1)}, f32[48,4096]{1,0:T(8,128)S(1)}) fusion(f32[4096]{0:T(1024)S(1)} %copy-done.8, f32[48,4096]{1,0:T(8,128)S(1)} %bitcast.100, bf16[48,4096]{1,0:T(8,128)(2,1)S(1)} %reshape.237, bf16[4096,4096]{1,0:T(8,128)(2,1)} %param.37), kind=kOutput, calls=%fused_computation.133 | convolution fusion | flops 1611595776 | bytes 35537088 | tf_op jit(solution)/shard_map/dot_general | solution.py:104
  331.2 0.3 multiply_reduce_fusion
  331.5 0.2 add_convert_fusion.1
  331.7 2.5 fusion.17
  334.2 0.2 fusion.100
  334.4 0.7 fusion.99
  335.3 8.6 %fusion.13 = f32[48,4096]{1,0:T(8,128)} fusion(bf16[16,30,4096]{2,0,1:T(8,128)(2,1)} %param.44, bf16[16,4096,30]{1,0,2:T(8,128)(2,1)} %param.43, bf16[48,4096]{1,0:T(8,128)(2,1)S(1)} %add_convert_fusion.1, f32[48,16,30]{0,2,1:T(8,128)S(1)} %fusion.17, f32[48,16]{0,1:T(8,128)S(1)} %copy.257), kind=kOutput, calls=%fused_computation.17 | convolution fusion | flops 378041856 | bytes 9139200 | tf_op jit(solution)/shard_map/bef,efd->bd/dot_general | solution.py:68
  344.0 0.7 copy.246
  344.6 0.7 copy_bitcast_fusion
  345.3 92.2 %all-reduce.2.cloned.1.call-done = f32[48,4096]{1,0:T(8,128)} async-done(((f32[48,4096]{1,0:T(8,128)}), f32[48,4096]{1,0:T(8,128)}) %all-reduce.2.cloned.1.call-update) | async-done | bytes 786448 | tf_op jit(solution)/shard_map/psum | solution.py:108
  437.5 1.9 add_convert_fusion
  (53 shorter events, 0.5 us)
Async XLA Ops:
  7.2 327.0 %copy-start = (bf16[4096,16]{0,1:T(8,128)(2,1)S(1)}, bf16[4096,16]{0,1:T(8,128)(2,1)}, u32[]{:S(2)}) copy-start(bf16[4096,16]{0,1:T(8,128)(2,1)} %param.41) | copy-start | bytes 393220
  7.2 198.1 %all-gather.3.cloned.1.call-start = ((), (), s32[]{:S(2)}) async-start(), calls=%async_computation.1 | async-start | bytes 51904512 | tf_op jit(solution)/shard_map/all_gather | solution.py:95
  25.4 1.5 copy-start.14
  25.4 1.5 copy-start.17
  43.5 5.4 %copy-start.11 = (f32[1024]{0:T(1024)S(1)}, f32[1024]{0:T(1024)}, u32[]{:S(2)}) copy-start(f32[1024]{0:T(1024)} %param.34) | copy-start | bytes 12292
  48.7 388.8 %all-reduce.2.cloned.1.call-start = ((), (), s32[]{:S(2)}) async-start(), calls=%async_computation | async-start | bytes 1572864 | tf_op jit(solution)/shard_map/psum | solution.py:108
  53.9 4.0 copy-start.12
  54.4 1.7 copy-start.6
  57.9 6.6 %copy-start.13 = (s32[3,16,2]{1,2,0:T(2,128)S(1)}, s32[3,16,2]{1,2,0:T(2,128)}, u32[]{:S(2)}) copy-start(s32[3,16,2]{1,2,0:T(2,128)} %param.46) | copy-start | bytes 1156
  57.9 6.7 %copy-start.1 = (bf16[2,16,4096]{2,1,0:T(8,128)(2,1)S(1)}, bf16[2,16,4096]{2,1,0:T(8,128)(2,1)}, u32[]{:S(2)}) copy-start(bf16[2,16,4096]{2,1,0:T(8,128)(2,1)} %param.25) | copy-start | bytes 786436
  57.9 6.7 %copy-start.4 = (bf16[16,4096]{1,0:T(8,128)(2,1)S(1)}, bf16[16,4096]{1,0:T(8,128)(2,1)}, u32[]{:S(2)}) copy-start(bf16[16,4096]{1,0:T(8,128)(2,1)} %param.24) | copy-start | bytes 393220
  300.9 4.8 %copy-start.5 = (f32[16,8,12]{1,2,0:T(8,128)S(1)}, f32[16,8,12]{1,2,0:T(8,128)}, u32[]{:S(2)}) copy-start(f32[16,8,12]{1,2,0:T(8,128)} %get-tuple-element.21) | copy-start | bytes 18436
  300.9 5.0 %copy-start.2 = (f32[1,16,8,12,128]{4,2,3,1,0:T(8,128)S(1)}, f32[1,16,8,12,128]{4,2,3,1,0:T(8,128)}, u32[]{:S(2)}) copy-start(f32[1,16,8,12,128]{4,2,3,1,0:T(8,128)} %copy.223) | copy-start | bytes 2359300
  305.9 11.0 %copy-start.3 = (f32[3,16,4096]{2,1,0:T(8,128)S(1)}, f32[3,16,4096]{2,1,0:T(8,128)}, u32[]{:S(2)}) copy-start(f32[3,16,4096]{2,1,0:T(8,128)} %fusion.93) | copy-start | bytes 2359300
  305.9 11.0 %copy-start.8 = (f32[4096]{0:T(1024)S(1)}, f32[4096]{0:T(1024)}, u32[]{:S(2)}) copy-start(f32[4096]{0:T(1024)} %param.38) | copy-start | bytes 49156
  317.0 14.4 %copy-start.9 = (f32[4096]{0:T(1024)S(1)}, f32[4096]{0:T(1024)}, u32[]{:S(2)}) copy-start(f32[4096]{0:T(1024)} %param.40) | copy-start | bytes 49156
  317.0 14.4 %copy-start.10 = (f32[4096]{0:T(1024)S(1)}, f32[4096]{0:T(1024)}, u32[]{:S(2)}) copy-start(f32[4096]{0:T(1024)} %param.39) | copy-start | bytes 49156
  317.0 14.6 %copy-start.15 = (bf16[16,4096,30]{1,0,2:T(8,128)(2,1)S(1)}, bf16[16,4096,30]{1,0,2:T(8,128)(2,1)}, u32[]{:S(2)}) copy-start(bf16[16,4096,30]{1,0,2:T(8,128)(2,1)} %param.42) | copy-start | bytes 11796484
  331.2 3.3 copy-start.16
  335.2 8.7 %copy-start.7 = (bf16[16,3,8,128]{3,2,0,1:T(8,128)(2,1)S(1)}, bf16[16,3,8,128]{3,2,0,1:T(8,128)(2,1)}, u32[]{:S(2)}) copy-start(bf16[16,3,8,128]{3,2,0,1:T(8,128)(2,1)} %copy-done.6) | copy-start | bytes 294916
Sparse Core Ops, SparseCore 0:
  48.8 156.4 all-gather.2
  344.1 93.3 all-reduce.1

commit v2 on v1

v2 whole, which is shorter than its diff:
```python
import functools
import math

import jax
import jax.numpy as jnp
import numpy as np
from jax import lax
from jax.experimental import pallas as pl
from jax.experimental.pallas import tpu as pltpu
from jax.sharding import PartitionSpec as P

ROPE_BASE = 10000.0
ROPE_MSCALE = math.sqrt(1.0 + math.log(32.0) / math.log(4096.0))
NORM_EPS = 1e-5
NEG_FILL = -1e30
MESH = pl.DeviceIdType.MESH
F32 = jnp.float32
BF16 = jnp.bfloat16
LANES = 128
WCOLS = 512
CORES = 2
VMEM_BYTES = 67043328
NT = (((1,), (1,)), ((), ()))


def iota(shape, dim):
    return lax.broadcasted_iota(jnp.int32, shape, dim)


def to_row(col):
    rows = col.shape[0]
    pick = iota((rows, LANES), 0) == iota((rows, LANES), 1)
    return jnp.sum(jnp.where(pick, jnp.broadcast_to(col, (rows, LANES)), 0.0), axis=0, keepdims=True)


def to_col(row, rows):
    pick = iota((rows, LANES), 0) == iota((rows, LANES), 1)
    return jnp.sum(jnp.where(pick, jnp.broadcast_to(row, (rows, LANES)), 0.0), axis=1, keepdims=True)


def stat_tile(m_row, l_row):
    r = iota((8, LANES), 0)
    return jnp.where(r == 0, jnp.broadcast_to(m_row, (8, LANES)), jnp.where(r == 1, jnp.broadcast_to(l_row, (8, LANES)), 0.0))


def softmax_part(s_raw, valid, scale):
    s = jnp.where(valid, s_raw * scale, NEG_FILL)
    m = jnp.max(s, axis=1, keepdims=True)
    w = jnp.where(valid, jnp.exp(s - m), 0.0)
    return m, jnp.sum(w, axis=1, keepdims=True), w.astype(BF16)


def round_bf16(x):
    return x.astype(BF16).astype(F32)


def kernel(dims, lens_ref, ei_ref, rm_ref,
           x_first, next_emb, k_hbm, v_hbm, g1, c1, w_q, b_q, w_k, b_k, w_v, b_v, w_o, b_o, g2, c2, w_r, w_g, w_u, w_d, lf, pw,
           out_ref, tk_ref, tv_ref,
           wring, kbuf, vbuf, wmoe, xin, x32, h, vg1, vc1, vg2, vc2, vbo, vbq, vbk, vbv, vlf, vpw, vwr,
           qbuf, cosb, sinb, kt, vt, tkv, psend, precv, omine, osend, orecv, oxs, lhs, xg, gs, ub, mine, mpsend, mprecv, mosend, morecv, yg, t32,
           wsem, ksem, vsem, msem, ssem, qx_s, qx_r, kx_s, kx_r, vx_s, vx_r, ps_s, ps_r, os_s, os_r, ox_s, ox_r,
           xa_s, xa_r, xf_s, mp_s, mp_r, mo_s, mo_r, ya_s, ya_r, yf_s):
    S, B, D, T, KH, HD, H, E, FE, chips = (dims[k] for k in ("S", "B", "D", "T", "KH", "HD", "H", "E", "FE", "chips"))
    R = S * B
    HH, KHH = H // CORES, KH // CORES
    half_cols = D // CORES
    QG = H // KH
    QR = S * HH
    MR = QR + 8
    PC = LANES * CORES
    FEP = wmoe.shape[1]
    scale = HD ** -0.5
    me = lax.axis_index("kv")
    chip = me // CORES
    c = lax.rem(me, CORES)
    partner = chip * CORES + (1 - c)

    def peer(ch):
        return ch * CORES + c

    bar = pltpu.get_barrier_semaphore()
    pl.semaphore_signal(bar, inc=1, device_id={"kv": partner}, device_id_type=MESH)

    def sig(i, _):
        pl.semaphore_signal(bar, inc=1, device_id={"kv": peer(lax.rem(chip + i, chips))}, device_id_type=MESH)
        return 0
    lax.fori_loop(1, chips, sig, 0)

    def wsrc(ci):
        if ci < 4:
            return w_q.at[:, pl.ds(pl.multiple_of(c * half_cols + ci * WCOLS, WCOLS), WCOLS)]
        if ci == 4:
            return w_k.at[:, pl.ds(pl.multiple_of(c * WCOLS, WCOLS), WCOLS)]
        if ci == 5:
            return w_v.at[:, pl.ds(pl.multiple_of(c * WCOLS, WCOLS), WCOLS)]
        return w_o.at[:, pl.ds(pl.multiple_of(c * half_cols + (ci - 6) * WCOLS, WCOLS), WCOLS)]

    def wcopy(ci):
        return pltpu.make_async_copy(wsrc(ci), wring.at[ci % 4], wsem.at[ci])

    smalls = [(x_first, xin.at[0]), (next_emb, xin.at[pl.ds(1, S - 1)]), (g1, vg1), (c1, vc1), (b_q, vbq), (b_k, vbk), (b_v, vbv),
              (lf, vlf), (pw, vpw), (g2, vg2), (c2, vc2), (b_o, vbo), (w_r, vwr)]
    small_copies = [pltpu.make_async_copy(a, b, ssem.at[i]) for i, (a, b) in enumerate(smalls)]
    for cp in small_copies[:9]:
        cp.start()
    for ci in range(4):
        wcopy(ci).start()
    for cp in small_copies[9:]:
        cp.start()

    def kcopy(b):
        return pltpu.make_async_copy(k_hbm.at[b], kbuf.at[b], ksem.at[b])

    def vcopy(b):
        return pltpu.make_async_copy(v_hbm.at[b], vbuf.at[b], vsem.at[b])

    moe_copies = [pltpu.make_async_copy(src, wmoe.at[i, pl.ds(0, FE)], msem.at[i]) for i, src in enumerate((w_g, w_u, w_d))]

    wmoe[2, FE:FEP, :] = jnp.zeros((FEP - FE, D), BF16)
    lhs[...] = jnp.zeros_like(lhs)
    gs[...] = jnp.zeros_like(gs)
    tkv[...] = jnp.zeros_like(tkv)

    row_b = lax.rem(iota((R, LANES), 0), B)
    pos = iota((R, LANES), 0) // B
    for b in range(B):
        pos = pos + jnp.where(row_b == b, lens_ref[b], 0)

    def layer_norm(s, gain, bias):
        x = x32[s * B:(s + 1) * B, :]
        mean = jnp.sum(x, axis=1, keepdims=True) / D
        cen = x - mean
        var = jnp.sum(cen * cen, axis=1, keepdims=True) / D
        h[s * B:(s + 1) * B, :] = (cen * lax.rsqrt(var + NORM_EPS) * gain[...] + bias[...]).astype(BF16)

    for cp in small_copies[:9]:
        cp.wait()
    for s in range(S):
        x32[s * B:(s + 1) * B, :] = xin[s].astype(F32)
        layer_norm(s, vg1, vc1)
    inv = 1.0 / (vlf[...] * vpw[...])
    ang = pos.astype(F32) * inv
    cosb[...] = jnp.cos(ang) * ROPE_MSCALE
    sn = jnp.sin(ang) * ROPE_MSCALE
    sinb[...] = jnp.where(iota((R, LANES), 1) < HD // 2, -sn, sn)

    def rotate(x):
        return round_bf16(x * cosb[...] + pltpu.roll(x, HD // 2, 1) * sinb[...])

    def q_chunk(ci, _):
        pltpu.make_async_copy(wsrc(0), wring.at[ci], wsem.at[ci]).wait()
        off = pl.multiple_of(c * half_cols + ci * WCOLS, WCOLS)
        y = jnp.dot(h[...], wring[ci], preferred_element_type=F32) + vbq[:, pl.ds(off, WCOLS)]
        y = round_bf16(y)
        for t in range(WCOLS // HD):
            r = rotate(y[:, t * HD:(t + 1) * HD])
            hh = ci * (WCOLS // HD) + t
            for s in range(S):
                qbuf[c, pl.ds(s * HH + hh, B, stride=QR), :] = r[s * B:(s + 1) * B, :]

        @pl.when(ci == 0)
        def _():
            wcopy(4).start()

        @pl.when(ci == 1)
        def _():
            wcopy(5).start()

            def kv_start(j, _):
                b = lax.rem(chip + 1 + j, chips)
                kcopy(b).start()
                vcopy(b).start()
                return 0
            lax.fori_loop(0, B, kv_start, 0)

        @pl.when(ci == 2)
        def _():
            wcopy(6).start()

        @pl.when(ci == 3)
        def _():
            wcopy(7).start()
        return 0
    lax.fori_loop(0, 4, q_chunk, 0)

    pl.semaphore_wait(bar, chips)

    def to_partner(src, dst, ss, rs):
        return pltpu.make_async_remote_copy(src, dst, ss, rs, device_id={"kv": partner}, device_id_type=MESH)

    q_x = to_partner(qbuf.at[c], qbuf.at[c], qx_s, qx_r)
    q_x.start()

    wcopy(4).wait()
    y = round_bf16(jnp.dot(h[...], wring[0], preferred_element_type=F32) + vbk[:, pl.ds(pl.multiple_of(c * WCOLS, WCOLS), WCOLS)])
    for t in range(KHH):
        kt[c, t, :, :] = rotate(y[:, t * HD:(t + 1) * HD])
    wcopy(8).start()
    wcopy(5).wait()
    y = round_bf16(jnp.dot(h[...], wring[1], preferred_element_type=F32) + vbv[:, pl.ds(pl.multiple_of(c * WCOLS, WCOLS), WCOLS)])
    for t in range(KHH):
        vt[c, t, :, :] = y[:, t * HD:(t + 1) * HD]
    wcopy(9).start()
    for cp in moe_copies:
        cp.start()
    k_x = to_partner(kt.at[c], kt.at[c], kx_s, kx_r)
    v_x = to_partner(vt.at[c], vt.at[c], vx_s, vx_r)
    k_x.start()
    v_x.start()

    q_x.wait_recv()
    row_hh = lax.rem(iota((QR, T * KH), 0), HH) // QG
    lane = iota((QR, T * KH), 1)
    lane_kh = lax.rem(lane, KH)

    def o_copy(b):
        return pltpu.make_async_remote_copy(osend.at[b], orecv.at[chip], os_s.at[b], os_r.at[chip],
                                            device_id={"kv": peer(b)}, device_id_type=MESH)

    def pair_combine(b, dst, di):
        to_partner(psend.at[b], precv.at[b], ps_s.at[b], ps_r.at[b]).wait_recv()
        m1, l1 = omine[b, QR:QR + 1, :], omine[b, QR + 1:QR + 2, :]
        m2, l2 = precv[b, QR:QR + 1, :], precv[b, QR + 1:QR + 2, :]
        top = jnp.maximum(m1, m2)
        f1, f2 = jnp.exp(m1 - top), jnp.exp(m2 - top)
        dst[di, 0:QR, :] = omine[b, 0:QR, :] * to_col(f1, QR) + precv[b, 0:QR, :] * to_col(f2, QR)
        dst[di, QR:MR, :] = stat_tile(top, l1 * f1 + l2 * f2)

    def attn_step(j, _):
        b = lax.rem(chip + 1 + j, chips)
        kcopy(b).wait()
        vcopy(b).wait()
        lim = (lens_ref[b] - me * T) * KH
        for which in range(2):
            half = 1 - c if which == 0 else c
            dst = psend if which == 0 else omine
            qb = qbuf[half, pl.ds(pl.multiple_of(b * QR, QR), QR), :].astype(BF16)
            sc = lax.dot_general(qb, kbuf[b], NT, preferred_element_type=F32)
            valid = (lane_kh == row_hh + half * KHH) & (lane < lim)
            m, l, w = softmax_part(sc, valid, scale)
            dst[b, 0:QR, :] = jnp.dot(w, vbuf[b], preferred_element_type=F32)
            dst[b, QR:MR, :] = stat_tile(to_row(m), to_row(l))
            if which == 0:
                to_partner(psend.at[b], precv.at[b], ps_s.at[b], ps_r.at[b]).start()

        @pl.when(j > 0)
        def _():
            pb = lax.rem(chip + j, chips)
            pair_combine(pb, osend, pb)
            o_copy(pb).start()
        return 0
    lax.fori_loop(0, B, attn_step, 0)
    pair_combine(chip, orecv, chip)

    for s in range(S):
        for t in range(KHH):
            tkv[0, s * KHH + t:s * KHH + t + 1, :] = kt[c, t, pl.ds(s * B + chip, 1), :]
            tkv[1, s * KHH + t:s * KHH + t + 1, :] = vt[c, t, pl.ds(s * B + chip, 1), :]
    TR = tkv.shape[1]
    qb = qbuf[c, pl.ds(pl.multiple_of(chip * QR, QR), QR), :].astype(BF16)
    sc = lax.dot_general(qb, tkv[0].astype(BF16), NT, preferred_element_type=F32)
    tr, tl = iota((QR, TR), 0), iota((QR, TR), 1)
    valid = (lax.rem(tl, KHH) == lax.rem(tr, HH) // QG) & (tl // KHH <= tr // HH) & (tl < S * KHH)
    m, l, w = softmax_part(sc, valid, scale)
    orecv[chips, 0:QR, :] = jnp.dot(w, tkv[1].astype(BF16), preferred_element_type=F32)
    orecv[chips, QR:MR, :] = stat_tile(to_row(m), to_row(l))

    def o_wait(i, _):
        src = lax.rem(chip + chips - i, chips)
        pltpu.make_async_remote_copy(osend.at[0], orecv.at[src], os_s.at[0], os_r.at[src],
                                     device_id={"kv": peer(src)}, device_id_type=MESH).wait_recv()
        return 0
    lax.fori_loop(1, chips, o_wait, 0)

    top = orecv[0, QR:QR + 1, :]
    for i in range(1, chips + 1):
        top = jnp.maximum(top, orecv[i, QR:QR + 1, :])
    tot = jnp.zeros((1, LANES), F32)
    acc = jnp.zeros((QR, LANES), F32)
    for i in range(chips + 1):
        f = jnp.exp(orecv[i, QR:QR + 1, :] - top)
        tot = tot + orecv[i, QR + 1:QR + 2, :] * f
        acc = acc + orecv[i, 0:QR, :] * to_col(f, QR)
    oxs[c, :, :] = round_bf16(acc / to_col(tot, QR))
    o_x = to_partner(oxs.at[c], oxs.at[c], ox_s, ox_r)
    o_x.start()
    o_x.wait_recv()
    for hf in range(CORES):
        for hh in range(HH):
            lhs[0:S, (hf * HH + hh) * HD:(hf * HH + hh + 1) * HD] = oxs[hf, pl.ds(hh, S, stride=HH), :]
    for cp in small_copies[9:]:
        cp.wait()

    ctiles = WCOLS // LANES
    my_slot = pl.multiple_of(me * QR, QR)

    def wo_chunk(jn, _):
        slot = lax.rem(jn + 2, 4)
        pltpu.make_async_copy(wsrc(0), wring.at[slot], wsem.at[jn + 6]).wait()
        off = pl.multiple_of(c * half_cols + jn * WCOLS, WCOLS)
        d = jnp.dot(lhs[...].astype(BF16), wring[slot], preferred_element_type=F32)
        for s in range(S):
            v = round_bf16(x32[pl.ds(s * B + chip, 1), pl.ds(off, WCOLS)] + d[s:s + 1, :] + vbo[:, pl.ds(off, WCOLS)])
            for t in range(ctiles):
                xg[pl.ds(my_slot + s * HH + jn * ctiles + t, 1), :] = v[:, t * LANES:(t + 1) * LANES]
        return 0
    lax.fori_loop(0, 4, wo_chunk, 0)

    def gather(buf, ss, rs, fs):
        def blk(slot):
            return buf.at[pl.ds(pl.multiple_of(slot * QR, QR), QR)]

        def cp(slot, sem, dev):
            return pltpu.make_async_remote_copy(blk(slot), blk(slot), sem, rs.at[slot], device_id={"kv": dev}, device_id_type=MESH)

        def send(i, _):
            cp(me, ss.at[i], peer(lax.rem(chip + i, chips))).start()
            return 0
        cp(me, ss.at[0], partner).start()
        lax.fori_loop(1, chips, send, 0)

        def fwd(i, _):
            slot = peer(lax.rem(chip + chips - i, chips))
            cp(slot, ss.at[0], partner).wait_recv()
            cp(slot, fs.at[i], partner).start()
            return 0
        lax.fori_loop(1, chips, fwd, 0)

        def other(i, _):
            slot = lax.rem(chip + chips - i, chips) * CORES + (1 - c)
            cp(slot, ss.at[0], partner).wait_recv()
            return 0
        lax.fori_loop(0, chips, other, 0)

        def drain():
            cp(me, ss.at[0], partner).wait_send()

            def dr(i, _):
                cp(me, ss.at[i], partner).wait_send()
                cp(me, fs.at[i], partner).wait_send()
                return 0
            lax.fori_loop(1, chips, dr, 0)
        return drain

    x_drain = gather(xg, xa_s, xa_r, xf_s)
    for s in range(S):
        for hf in range(CORES):
            for t in range(HH):
                x32[s * B:(s + 1) * B, (hf * HH + t) * LANES:(hf * HH + t + 1) * LANES] = xg[pl.ds(hf * QR + s * HH + t, B, stride=CORES * QR), :]

    for s in range(S):
        layer_norm(s, vg2, vc2)
    logits = lax.dot_general(h[...], vwr[...], NT, preferred_element_type=F32)
    le = iota((B, E), 1)
    diag = iota((B, B), 0) == iota((B, B), 1)
    for s in range(S):
        lg = logits[s * B:(s + 1) * B, :]
        gate = jnp.zeros((B, E), F32)
        for k in range(ei_ref.shape[1]):
            masked = jnp.where(rm_ref[s, :, k, :] == 1, lg, NEG_FILL)
            ex = jnp.exp(masked - jnp.max(masked, axis=1, keepdims=True))
            p = ex / jnp.sum(ex, axis=1, keepdims=True)
            idx = jnp.sum(jnp.where(diag, jnp.broadcast_to(ei_ref[s, k:k + 1, :], (B, B)).astype(F32), 0.0), axis=1, keepdims=True)
            gate = gate + jnp.where(le.astype(F32) == idx, p, 0.0)
        gs[s * B:(s + 1) * B, 0:E] = gate
    g = gs[...]
    step = E
    while step < LANES:
        g = g + pltpu.roll(g, step, 1)
        step *= 2
    moe_copies[0].wait()
    moe_copies[1].wait()
    for t in range(FEP // 256):
        ag = lax.dot_general(h[...], wmoe[0, t * 256:(t + 1) * 256, :], NT, preferred_element_type=F32)
        au = lax.dot_general(h[...], wmoe[1, t * 256:(t + 1) * 256, :], NT, preferred_element_type=F32)
        gg = jnp.concatenate([g] * (256 // LANES), axis=1)
        u = gg * (ag * jax.nn.sigmoid(ag)) * au
        u = jnp.where(iota((R, 256), 1) + t * 256 < FE, u, 0.0)
        ub[:, t * 256:(t + 1) * 256] = u.astype(BF16)
    moe_copies[2].wait()

    def mo_copy(i):
        return pltpu.make_async_remote_copy(mosend.at[i], morecv.at[chip], mo_s.at[i], mo_r.at[chip],
                                            device_id={"kv": peer(i)}, device_id_type=MESH)

    def moe_pair(i, dst, di):
        to_partner(mpsend.at[i], mprecv.at[i], mp_s.at[i], mp_r.at[i]).wait_recv()
        dst[di, :, :] = mine[i] + mprecv[i]

    def moe_step(j, _):
        i = lax.rem(chip + 1 + j, chips)
        pp = round_bf16(jnp.dot(ub[...], wmoe[2, :, pl.ds(pl.multiple_of(i * PC, PC), PC)], preferred_element_type=F32))
        p0, p1 = pp[:, :LANES], pp[:, LANES:]
        mpsend[i, :, :] = jnp.where(c == 0, p1, p0)
        mine[i, :, :] = jnp.where(c == 0, p0, p1)
        to_partner(mpsend.at[i], mprecv.at[i], mp_s.at[i], mp_r.at[i]).start()

        @pl.when(j > 0)
        def _():
            pi = lax.rem(chip + j, chips)
            moe_pair(pi, mosend, pi)
            mo_copy(pi).start()
        return 0
    lax.fori_loop(0, chips, moe_step, 0)
    moe_pair(chip, morecv, chip)

    k_x.wait_recv()
    v_x.wait_recv()
    for src, dst in ((kt, tk_ref), (vt, tv_ref)):
        for hf in range(CORES):
            for t in range(KHH):
                for s in range(S):
                    t32[pl.ds(s * KH + hf * KHH + t, B, stride=S * KH), :] = src[hf, t, s * B:(s + 1) * B, :]
        dst[...] = t32[...].astype(BF16)

    def mo_wait(i, _):
        src = lax.rem(chip + chips - i, chips)
        pltpu.make_async_remote_copy(mosend.at[0], morecv.at[src], mo_s.at[0], mo_r.at[src],
                                     device_id={"kv": peer(src)}, device_id_type=MESH).wait_recv()
        return 0
    lax.fori_loop(1, chips, mo_wait, 0)
    tot = morecv[0]
    for i in range(1, chips):
        tot = tot + morecv[i]
    yg[pl.ds(my_slot, QR), :] = round_bf16(x32[:, pl.ds(pl.multiple_of(me * LANES, LANES), LANES)] + tot)
    y_drain = gather(yg, ya_s, ya_r, yf_s)
    for d in range(chips * CORES):
        for s in range(S):
            out_ref[s, :, d * LANES:(d + 1) * LANES] = yg[d * QR + s * B:d * QR + (s + 1) * B, :].astype(BF16)

    q_x.wait_send()
    k_x.wait_send()
    v_x.wait_send()
    o_x.wait_send()

    def drain(i, _):
        b = lax.rem(chip + i, chips)
        to_partner(psend.at[b], precv.at[b], ps_s.at[b], ps_r.at[b]).wait_send()
        to_partner(mpsend.at[b], mprecv.at[b], mp_s.at[b], mp_r.at[b]).wait_send()

        @pl.when(i > 0)
        def _():
            o_copy(b).wait_send()
            mo_copy(b).wait_send()
        return 0
    lax.fori_loop(0, chips, drain, 0)
    x_drain()
    y_drain()


def solution(mesh):
    n = mesh.shape["kv"]
    chips = n // CORES

    def layer_steps(x_first, next_emb, k_cache, v_cache, seq_len, ln1_gain, ln1_bias, w_q, b_q, w_k, b_k, w_v, b_v, w_o, b_o, ln2_gain, ln2_bias, w_router, w_gate, w_up, w_down, long_factor, expert_idx, route_mask):
        B, T, KH, HD = k_cache.shape
        D = x_first.shape[1]
        H = w_q.shape[1] // HD
        S = next_emb.shape[0] + 1
        E = w_router.shape[1]
        FE = w_gate.shape[0] * w_gate.shape[2]
        FEP = -(-FE // 256) * 256
        R = S * B
        HH, KHH = H // CORES, KH // CORES
        QR = S * HH
        MR = QR + 8
        if B != chips or D != n * LANES or w_q.shape[1] != D or QR != R:
            raise ValueError("unsupported sizes")
        dims = dict(S=S, B=B, D=D, T=T, KH=KH, HD=HD, H=H, E=E, FE=FE, chips=chips)
        half = HD // 2
        power = np.float32(ROPE_BASE) ** (np.arange(half, dtype=np.float32) * np.float32(2.0) / np.float32(HD))
        pw = jnp.asarray(np.concatenate([power, power])[None, :].astype(np.float32))
        lf = jnp.concatenate([long_factor, long_factor])[None, :]
        row = lambda a: a.reshape(1, -1)
        args = (seq_len, expert_idx.transpose(0, 2, 1), route_mask,
                x_first, next_emb, k_cache.reshape(B, T * KH, HD), v_cache.reshape(B, T * KH, HD), row(ln1_gain), row(ln1_bias),
                w_q, row(b_q), w_k, row(b_k), w_v, row(b_v), w_o, row(b_o), row(ln2_gain), row(ln2_bias), w_router.T,
                w_gate.transpose(2, 0, 1).reshape(FE, D), w_up.transpose(2, 0, 1).reshape(FE, D), w_down.transpose(1, 0, 2).reshape(FE, D), lf, pw)
        V = pltpu.VMEM
        DS = pltpu.SemaphoreType.DMA
        scratch = [
            V((4, D, WCOLS), BF16), V((B, T * KH, HD), BF16), V((B, T * KH, HD), BF16), V((3, FEP, D), BF16),
            V((S, B, D), BF16), V((R, D), F32), V((R, D), BF16),
            V((1, D), F32), V((1, D), F32), V((1, D), F32), V((1, D), F32), V((1, D), F32), V((1, w_q.shape[1]), F32),
            V((1, w_k.shape[1]), F32), V((1, w_v.shape[1]), F32), V((1, HD), F32), V((1, HD), F32), V((E, D), BF16),
            V((CORES, B * QR, HD), F32), V((R, HD), F32), V((R, HD), F32), V((CORES, KHH, R, HD), F32), V((CORES, KHH, R, HD), F32), V((2, 16, HD), F32),
            V((B, MR, HD), F32), V((B, MR, HD), F32), V((B, MR, HD), F32), V((B, MR, HD), F32), V((chips + 1, MR, HD), F32),
            V((CORES, QR, HD), F32), V((8, D), F32), V((n * QR, HD), F32), V((R, LANES), F32), V((R, FEP), BF16),
            V((chips, R, LANES), F32), V((chips, R, LANES), F32), V((chips, R, LANES), F32), V((chips, R, LANES), F32), V((chips, R, LANES), F32),
            V((n * QR, LANES), F32), V((B * S * KH, HD), F32),
            DS((10,)), DS((B,)), DS((B,)), DS((3,)), DS((13,)), DS, DS, DS, DS, DS, DS, DS((B,)), DS((B,)), DS((chips,)), DS((chips,)), DS, DS,
            DS((chips,)), DS((n,)), DS((chips,)), DS((chips,)), DS((chips,)), DS((chips,)), DS((chips,)), DS((chips,)), DS((n,)), DS((chips,)),
        ]
        vm = pl.BlockSpec(memory_space=pltpu.VMEM)
        anys = pl.BlockSpec(memory_space=pl.ANY)
        hidden, tk, tv = pl.pallas_call(
            functools.partial(kernel, dims),
            name="decode_layer",
            out_shape=(jax.ShapeDtypeStruct((S, B, D), BF16), jax.ShapeDtypeStruct((B * S * KH, HD), BF16), jax.ShapeDtypeStruct((B * S * KH, HD), BF16)),
            in_specs=[pl.BlockSpec(memory_space=pltpu.SMEM), vm, vm] + [anys] * (len(args) - 3),
            out_specs=(vm, vm, vm),
            scratch_shapes=scratch,
            compiler_params=pltpu.CompilerParams(collective_id=0, has_side_effects=True, vmem_limit_bytes=VMEM_BYTES),
        )(*args)
        return hidden, tk.reshape(B, S, KH, HD), tv.reshape(B, S, KH, HD)

    replicated = P()
    in_specs = (P('dp'), P(None, 'dp'), P('dp', 'kv'), P('dp', 'kv'), P('dp')) + (replicated,) * 13 + (P(None, None, 'kv'), P(None, None, 'kv'), P(None, 'kv'), replicated, P(None, 'dp'), P(None, 'dp'))
    out_specs = (P(None, 'dp'), P('dp'), P('dp'))
    return jax.shard_map(layer_steps, mesh=mesh, in_specs=in_specs, out_specs=out_specs, check_vma=False)
```

time: 450 us -> 90.2 us (0.20)
  waiting for transfers between devices: 232 us -> 0 us
  Pallas kernels: 0 us -> 83.1 us
  local copies, waits for them, and re-layouts: 77.6 us -> 4.85 us
  matrix products: 61.6 us -> 0 us
  other arithmetic: 60.3 us -> 1.32 us
  between operations: 15 us -> 0.64 us
    all_gather x1 -> x0, waiting for transfers between devices: 140 us -> none  [layer_steps(): gathered = lax.all_gather(packed, 'kv')]
    psum x1 -> x0, waiting for transfers between devices: 92.2 us -> none  [layer_steps(): moe_sum = lax.psum(moe_part.astype(jnp.float32), 'kv')]
    pallas_call x0 -> x1, Pallas kernels: none -> 83.1 us  [layer_steps(): pl.pallas_call(functools.partial(kernel, dims), name='decode_layer', out_...]
    dot_general x10 -> x0, matrix products: 61.3 us -> none  [the longest x1 14.1 us: layer_steps(): jnp.dot(attn, w_o, preferred_element_type=jnp.float32)]
    slice x4 -> x0, local copies, waits for them, and re-layouts: 59.4 us -> none  [the longest x1 24.6 us: layer_steps(): out_all = jnp.concatenate([gathered[..., 2:], tail_out[None]], axis=0)]
    slice x1 -> x0, other arithmetic: 33.6 us -> none  [layer_steps(): max_all = jnp.concatenate([gathered[..., 0], tail_max[None]], axis=0)]
    reduce_sum x7 -> x0, other arithmetic: 16.9 us -> none  [the longest x1 10.3 us: combine_stats(): merged = jnp.sum(out_all * factor[..., None], axis=0)]
    broadcast_in_dim x6 -> x0, local copies, waits for them, and re-layouts: 5.04 us -> none  [the longest x1 1.92 us: layer_steps(): run_sum[..., None]]
  transfers between devices with their start and end apart: 2 -> 0, of which waited for: 2 -> 0; matrix products, arithmetic and copies ran while one was open for 4% -> 0% of each run, Pallas kernels for 0% -> 0%
where the time goes in v2:
time: 90.2 us; the launch traced here: 89.9 us
  Pallas kernels  83.1 us (92%)
  local copies, waits for them, and re-layouts  4.85 us (5%)
  other arithmetic  1.32 us (1%)
    pallas_call x1, Pallas kernels, layer_steps(): pl.pallas_call(functools.partial(kernel, dims), name='decode_layer', out_...  83.1 us
    unnamed x3, local copies, waits for them, and re-layouts  4.85 us

profile of v2, /device:TPU:97, one launch (start us, length us, event | category | flops | bytes accessed | tf_op | source)
XLA Modules:
  0.0 89.9 jit_solution(10504980497516913753)
XLA Ops:
  0.6 1.3 %maximum_bitcast_fusion.lf = f32[1,128]{1,0:T(1,128)} fusion(f32[64]{0:T(128)} %param.46), kind=kLoop, calls=%fused_computation | loop fusion | flops 128 | bytes 768 | tf_op jit(solution)/shard_map/broadcast_in_dim | solution.py:474
  1.9 83.1 %decode_layer.1 = (bf16[3,16,4096]{2,1,0:T(8,128)(2,1)}, bf16[384,128]{1,0:T(8,128)(2,1)}, bf16[384,128]{1,0:T(8,128)(2,1)}) custom-call(s32[16]{0:T(128)} %lens_ref.1, s32[3,2,16]{2,1,0:T(2,128)} %bitcast.41, s32[3,16,2,16]{3,2,1,0:T(2,128)} %rm_ref.1, bf16[16,4096]{1,0:T(8,128)(2,1)} %x_first.1, bf16[2,16,4096]{2,1,0:T(8,128)(2,1)} %next_emb.1, ...), custom_call_target="tpu_custom_call" | custom-call | tf_op jit(solution)/shard_map/decode_layer/pallas_call | solution.py:497
  85.1 1.8 %copy.31 = bf16[3,16,4096]{2,1,0:T(8,128)(2,1)} copy(bf16[3,16,4096]{2,1,0:T(8,128)(2,1)} %get-tuple-element.12) | data formatting | bytes 786432
  86.8 1.5 %copy.32 = bf16[16,3,8,128]{3,2,1,0:T(8,128)(2,1)} copy(bf16[16,3,8,128]{3,2,1,0:T(8,128)(2,1)} %bitcast.32) | data formatting | bytes 196608
  88.4 1.5 %copy.33 = bf16[16,3,8,128]{3,2,1,0:T(8,128)(2,1)} copy(bf16[16,3,8,128]{3,2,1,0:T(8,128)(2,1)} %bitcast.31) | data formatting | bytes 196608

commit v3 on v2

--- a/solution.py
+++ b/solution.py
@@ -19,7 +19,7 @@
 LANES = 128
 WCOLS = 512
 CORES = 2
-VMEM_BYTES = 67043328
+VMEM_BYTES = 64 * 1024 * 1024 - 4 * 1024 * 1024
 NT = (((1,), (1,)), ((), ()))
 
 
@@ -54,11 +54,11 @@
     return x.astype(BF16).astype(F32)
 
 
-def kernel(dims, lens_ref, ei_ref, rm_ref,
+def kernel(dims, lens_h, ei_h, rm_h,
            x_first, next_emb, k_hbm, v_hbm, g1, c1, w_q, b_q, w_k, b_k, w_v, b_v, w_o, b_o, g2, c2, w_r, w_g, w_u, w_d, lf, pw,
            out_ref, tk_ref, tv_ref,
-           wring, kbuf, vbuf, wmoe, xin, x32, h, vg1, vc1, vg2, vc2, vbo, vbq, vbk, vbv, vlf, vpw, vwr,
-           qbuf, cosb, sinb, kt, vt, tkv, psend, precv, omine, osend, orecv, oxs, lhs, xg, gs, ub, mine, mpsend, mprecv, mosend, morecv, yg, t32,
+           lens_ref, ei_ref, rm_ref, wring, kbuf, vbuf, wmoe, xin, x32, h, vg1, vc1, vg2, vc2, vbo, vbq, vbk, vbv, vlf, vpw, vwr,
+           qbuf, cosb, sinb, kt, vt, tkv, kbias, sbuf, wbuf, part, precv, osend, orecv, oxs, lhs, wacc, xg, gs, gt, ut, ub, mine, mpsend, mprecv, mosend, morecv, yg, t32,
            wsem, ksem, vsem, msem, ssem, qx_s, qx_r, kx_s, kx_r, vx_s, vx_r, ps_s, ps_r, os_s, os_r, ox_s, ox_r,
            xa_s, xa_r, xf_s, mp_s, mp_r, mo_s, mo_r, ya_s, ya_r, yf_s):
     S, B, D, T, KH, HD, H, E, FE, chips = (dims[k] for k in ("S", "B", "D", "T", "KH", "HD", "H", "E", "FE", "chips"))
@@ -79,6 +79,25 @@
     def peer(ch):
         return ch * CORES + c
 
+    side = math.isqrt(chips)
+    cy, cx = chip // side, lax.rem(chip, side)
+
+    def ring(k):
+        return side // 2 + ((k + 1) // 2) * (1 - 2 * (k % 2))
+
+    def nth(j):
+        return lax.rem(cy + ring(j // side), side) * side + lax.rem(cx + ring(lax.rem(j, side)), side)
+
+    def dist(d):
+        return min(d, side - d)
+    offsets = sorted([(dy, dx) for dy in range(side) for dx in range(side) if dy or dx], key=lambda o: -(dist(o[0]) + dist(o[1])))
+
+    def ahead(o):
+        return lax.rem(cy + o[0], side) * side + lax.rem(cx + o[1], side)
+
+    def behind(o):
+        return lax.rem(cy + side - o[0], side) * side + lax.rem(cx + side - o[1], side)
+
     bar = pltpu.get_barrier_semaphore()
     pl.semaphore_signal(bar, inc=1, device_id={"kv": partner}, device_id_type=MESH)
 
@@ -100,13 +119,13 @@
         return pltpu.make_async_copy(wsrc(ci), wring.at[ci % 4], wsem.at[ci])
 
     smalls = [(x_first, xin.at[0]), (next_emb, xin.at[pl.ds(1, S - 1)]), (g1, vg1), (c1, vc1), (b_q, vbq), (b_k, vbk), (b_v, vbv),
-              (lf, vlf), (pw, vpw), (g2, vg2), (c2, vc2), (b_o, vbo), (w_r, vwr)]
+              (lf, vlf), (pw, vpw), (lens_h, lens_ref), (g2, vg2), (c2, vc2), (b_o, vbo), (w_r, vwr), (ei_h, ei_ref), (rm_h, rm_ref)]
     small_copies = [pltpu.make_async_copy(a, b, ssem.at[i]) for i, (a, b) in enumerate(smalls)]
-    for cp in small_copies[:9]:
+    for cp in small_copies[:10]:
         cp.start()
     for ci in range(4):
         wcopy(ci).start()
-    for cp in small_copies[9:]:
+    for cp in small_copies[10:]:
         cp.start()
 
     def kcopy(b):
@@ -120,12 +139,8 @@
     wmoe[2, FE:FEP, :] = jnp.zeros((FEP - FE, D), BF16)
     lhs[...] = jnp.zeros_like(lhs)
     gs[...] = jnp.zeros_like(gs)
+    ut[...] = jnp.zeros_like(ut)
     tkv[...] = jnp.zeros_like(tkv)
-
-    row_b = lax.rem(iota((R, LANES), 0), B)
-    pos = iota((R, LANES), 0) // B
-    for b in range(B):
-        pos = pos + jnp.where(row_b == b, lens_ref[b], 0)
 
     def layer_norm(s, gain, bias):
         x = x32[s * B:(s + 1) * B, :]
@@ -134,16 +149,25 @@
         var = jnp.sum(cen * cen, axis=1, keepdims=True) / D
         h[s * B:(s + 1) * B, :] = (cen * lax.rsqrt(var + NORM_EPS) * gain[...] + bias[...]).astype(BF16)
 
-    for cp in small_copies[:9]:
+    for cp in small_copies[:10]:
         cp.wait()
     for s in range(S):
         x32[s * B:(s + 1) * B, :] = xin[s].astype(F32)
         layer_norm(s, vg1, vc1)
-    inv = 1.0 / (vlf[...] * vpw[...])
-    ang = pos.astype(F32) * inv
-    cosb[...] = jnp.cos(ang) * ROPE_MSCALE
+    hd2 = HD // 2
+    row_b = lax.rem(iota((R, hd2), 0), B)
+    pos = iota((R, hd2), 0) // B
+    for b in range(B):
+        pos = pos + jnp.where(row_b == b, lens_ref[b], 0)
+    ang = pos.astype(F32) * (1.0 / (vlf[...] * vpw[...]))
+    cs = jnp.cos(ang) * ROPE_MSCALE
     sn = jnp.sin(ang) * ROPE_MSCALE
-    sinb[...] = jnp.where(iota((R, LANES), 1) < HD // 2, -sn, sn)
+    cosb[:, 0:hd2] = cs
+    cosb[:, hd2:HD] = cs
+    sinb[:, 0:hd2] = -sn
+    sinb[:, hd2:HD] = sn
+    kr, kl = iota((CORES * QR, LANES), 0), iota((CORES * QR, LANES), 1)
+    kbias[...] = jnp.where((kr // QR) * KHH + lax.rem(kr, HH) // QG == lax.rem(kl, KH), 0.0, NEG_FILL)
 
     def rotate(x):
         return round_bf16(x * cosb[...] + pltpu.roll(x, HD // 2, 1) * sinb[...])
@@ -168,7 +192,7 @@
             wcopy(5).start()
 
             def kv_start(j, _):
-                b = lax.rem(chip + 1 + j, chips)
+                b = nth(j)
                 kcopy(b).start()
                 vcopy(b).start()
                 return 0
@@ -210,47 +234,82 @@
     v_x.start()
 
     q_x.wait_recv()
-    row_hh = lax.rem(iota((QR, T * KH), 0), HH) // QG
-    lane = iota((QR, T * KH), 1)
-    lane_kh = lax.rem(lane, KH)
+    AR = CORES * QR
+    NK = T * KH
+    fac = scale * math.log2(math.e)
+    lane = iota((AR, LANES), 1)
 
     def o_copy(b):
         return pltpu.make_async_remote_copy(osend.at[b], orecv.at[chip], os_s.at[b], os_r.at[chip],
                                             device_id={"kv": peer(b)}, device_id_type=MESH)
 
+    def p_copy(b):
+        return to_partner(part.at[1 - c, b], precv.at[b], ps_s.at[b], ps_r.at[b])
+
     def pair_combine(b, dst, di):
-        to_partner(psend.at[b], precv.at[b], ps_s.at[b], ps_r.at[b]).wait_recv()
-        m1, l1 = omine[b, QR:QR + 1, :], omine[b, QR + 1:QR + 2, :]
+        p_copy(b).wait_recv()
+        m1, l1 = part[c, b, QR:QR + 1, :], part[c, b, QR + 1:QR + 2, :]
         m2, l2 = precv[b, QR:QR + 1, :], precv[b, QR + 1:QR + 2, :]
         top = jnp.maximum(m1, m2)
         f1, f2 = jnp.exp(m1 - top), jnp.exp(m2 - top)
-        dst[di, 0:QR, :] = omine[b, 0:QR, :] * to_col(f1, QR) + precv[b, 0:QR, :] * to_col(f2, QR)
+        dst[di, 0:QR, :] = part[c, b, 0:QR, :] * to_col(f1, QR) + precv[b, 0:QR, :] * to_col(f2, QR)
         dst[di, QR:MR, :] = stat_tile(top, l1 * f1 + l2 * f2)
 
-    def attn_step(j, _):
-        b = lax.rem(chip + 1 + j, chips)
-        kcopy(b).wait()
-        vcopy(b).wait()
+    def scores(b, u):
         lim = (lens_ref[b] - me * T) * KH
-        for which in range(2):
-            half = 1 - c if which == 0 else c
-            dst = psend if which == 0 else omine
-            qb = qbuf[half, pl.ds(pl.multiple_of(b * QR, QR), QR), :].astype(BF16)
-            sc = lax.dot_general(qb, kbuf[b], NT, preferred_element_type=F32)
-            valid = (lane_kh == row_hh + half * KHH) & (lane < lim)
-            m, l, w = softmax_part(sc, valid, scale)
-            dst[b, 0:QR, :] = jnp.dot(w, vbuf[b], preferred_element_type=F32)
-            dst[b, QR:MR, :] = stat_tile(to_row(m), to_row(l))
-            if which == 0:
-                to_partner(psend.at[b], precv.at[b], ps_s.at[b], ps_r.at[b]).start()
-
-        @pl.when(j > 0)
-        def _():
-            pb = lax.rem(chip + j, chips)
-            pair_combine(pb, osend, pb)
-            o_copy(pb).start()
-        return 0
-    lax.fori_loop(0, B, attn_step, 0)
+        q0 = qbuf[0, pl.ds(pl.multiple_of(b * QR, QR), QR), :]
+        q1 = qbuf[1, pl.ds(pl.multiple_of(b * QR, QR), QR), :]
+        qb = jnp.concatenate([q0, q1], axis=0).astype(BF16)
+        mx = jnp.full((AR, LANES), NEG_FILL, F32)
+        for col in range(NK // 256):
+            x = lax.dot_general(qb, kbuf[b, col * 256:(col + 1) * 256, :], NT, preferred_element_type=F32)
+            for hc in range(256 // LANES):
+                lo = col * 256 + hc * LANES
+                xx = jnp.where(lane < lim - lo, x[:, hc * LANES:(hc + 1) * LANES] + kbias[...], NEG_FILL)
+                sbuf[u, :, lo:lo + LANES] = xx
+                mx = jnp.maximum(mx, xx)
+        m = jnp.max(mx, axis=1, keepdims=True)
+        mu = jnp.where(lim > 0, m, 0.0)
+        return m, mu
+
+    def weigh(b, u, m, mu):
+        mub = jnp.broadcast_to(mu, (AR, LANES))
+        tot = jnp.zeros((AR, LANES), F32)
+        for lo in range(0, NK, LANES):
+            w = jnp.exp2((sbuf[u, :, lo:lo + LANES] - mub) * fac)
+            tot = tot + w
+            wbuf[u, :, lo:lo + LANES] = w.astype(BF16)
+        l = jnp.sum(tot, axis=1, keepdims=True)
+        o = jnp.dot(wbuf[u], vbuf[b], preferred_element_type=F32)
+        ms = m * scale
+        for hf in range(CORES):
+            part[hf, b, 0:QR, :] = o[hf * QR:(hf + 1) * QR, :]
+            part[hf, b, QR:MR, :] = stat_tile(to_row(ms[hf * QR:(hf + 1) * QR, :]), to_row(l[hf * QR:(hf + 1) * QR, :]))
+
+    def attn2(jj):
+        bs = [nth(jj * 2 + u) for u in range(2)]
+        for b in bs:
+            kcopy(b).wait()
+            vcopy(b).wait()
+        st = [scores(b, u) for u, b in enumerate(bs)]
+        for u, b in enumerate(bs):
+            weigh(b, u, *st[u])
+        for b in bs:
+            p_copy(b).start()
+
+    def comb(b):
+        pair_combine(b, osend, b)
+        o_copy(b).start()
+
+    attn2(0)
+
+    def attn_step(jj, _):
+        attn2(jj)
+        comb(nth(jj * 2 - 2))
+        comb(nth(jj * 2 - 1))
+        return 0
+    lax.fori_loop(1, B // 2, attn_step, 0)
+    comb(nth(B - 2))
     pair_combine(chip, orecv, chip)
 
     for s in range(S):
@@ -267,7 +326,7 @@
     orecv[chips, QR:MR, :] = stat_tile(to_row(m), to_row(l))
 
     def o_wait(i, _):
-        src = lax.rem(chip + chips - i, chips)
+        src = lax.rem(chip + i, chips)
         pltpu.make_async_remote_copy(osend.at[0], orecv.at[src], os_s.at[0], os_r.at[src],
                                      device_id={"kv": peer(src)}, device_id_type=MESH).wait_recv()
         return 0
@@ -285,69 +344,82 @@
     oxs[c, :, :] = round_bf16(acc / to_col(tot, QR))
     o_x = to_partner(oxs.at[c], oxs.at[c], ox_s, ox_r)
     o_x.start()
-    o_x.wait_recv()
-    for hf in range(CORES):
-        for hh in range(HH):
-            lhs[0:S, (hf * HH + hh) * HD:(hf * HH + hh + 1) * HD] = oxs[hf, pl.ds(hh, S, stride=HH), :]
-    for cp in small_copies[9:]:
+    for cp in small_copies[10:]:
         cp.wait()
 
     ctiles = WCOLS // LANES
     my_slot = pl.multiple_of(me * QR, QR)
-
-    def wo_chunk(jn, _):
-        slot = lax.rem(jn + 2, 4)
-        pltpu.make_async_copy(wsrc(0), wring.at[slot], wsem.at[jn + 6]).wait()
-        off = pl.multiple_of(c * half_cols + jn * WCOLS, WCOLS)
-        d = jnp.dot(lhs[...].astype(BF16), wring[slot], preferred_element_type=F32)
-        for s in range(S):
-            v = round_bf16(x32[pl.ds(s * B + chip, 1), pl.ds(off, WCOLS)] + d[s:s + 1, :] + vbo[:, pl.ds(off, WCOLS)])
-            for t in range(ctiles):
-                xg[pl.ds(my_slot + s * HH + jn * ctiles + t, 1), :] = v[:, t * LANES:(t + 1) * LANES]
-        return 0
-    lax.fori_loop(0, 4, wo_chunk, 0)
-
-    def gather(buf, ss, rs, fs):
-        def blk(slot):
-            return buf.at[pl.ds(pl.multiple_of(slot * QR, QR), QR)]
-
-        def cp(slot, sem, dev):
-            return pltpu.make_async_remote_copy(blk(slot), blk(slot), sem, rs.at[slot], device_id={"kv": dev}, device_id_type=MESH)
-
-        def send(i, _):
-            cp(me, ss.at[i], peer(lax.rem(chip + i, chips))).start()
+    KROWS = HH * HD
+
+    def fill(hf):
+        for hh in range(HH):
+            lhs[hf, 0:S, hh * HD:(hh + 1) * HD] = oxs[hf, pl.ds(hh, S, stride=HH), :]
+
+    def wo_dot(hf, jn):
+        return jnp.dot(lhs[hf].astype(BF16), wring[lax.rem(jn + 2, 4), pl.ds(pl.multiple_of(hf * KROWS, KROWS), KROWS), :], preferred_element_type=F32)
+
+    fill(c)
+
+    def wo_mine(jn, _):
+        pltpu.make_async_copy(wsrc(0), wring.at[lax.rem(jn + 2, 4)], wsem.at[jn + 6]).wait()
+        wacc[jn, :, :] = wo_dot(c, jn)
+        return 0
+    lax.fori_loop(0, 4, wo_mine, 0)
+    o_x.wait_recv()
+    fill(1 - c)
+
+    def gatherer(buf, pieces, ss, rs, fs):
+        PR = QR // pieces
+
+        def cp(p, slot, sem, dev):
+            blk = buf.at[pl.ds(pl.multiple_of(slot * QR + p * PR, 8), PR)]
+            return pltpu.make_async_remote_copy(blk, blk, sem, rs.at[p, slot], device_id={"kv": dev}, device_id_type=MESH)
+
+        def send(p):
+            for i, o in enumerate(offsets):
+                cp(p, me, ss.at[p, i], peer(ahead(o))).start()
+            cp(p, me, ss.at[p, len(offsets)], partner).start()
+
+        def finish():
+            for p in range(pieces):
+                for i, o in enumerate(offsets):
+                    slot = peer(behind(o))
+                    cp(p, slot, ss.at[p, i], partner).wait_recv()
+                    cp(p, slot, fs.at[p, i], partner).start()
+            for p in range(pieces):
+                cp(p, partner, ss.at[p, 0], partner).wait_recv()
+                for i, o in enumerate(offsets):
+                    cp(p, behind(o) * CORES + (1 - c), ss.at[p, i], partner).wait_recv()
+
+        def drain():
+            for p in range(pieces):
+                cp(p, me, ss.at[p, len(offsets)], partner).wait_send()
+                for i in range(len(offsets)):
+                    cp(p, me, ss.at[p, i], partner).wait_send()
+                    cp(p, me, fs.at[p, i], partner).wait_send()
+        return send, finish, drain
+
+    XP = 2
+    XPR = QR // XP
+    XT = HH // XP
+    x_send, x_finish, x_drain = gatherer(xg, XP, xa_s, xa_r, xf_s)
+    for p in range(XP):
+        def wo_other(k, _):
+            jn = p * (4 // XP) + k
+            off = pl.multiple_of(c * half_cols + jn * WCOLS, WCOLS)
+            d = wacc[jn] + wo_dot(1 - c, jn)
+            for s in range(S):
+                v = round_bf16(x32[pl.ds(s * B + chip, 1), pl.ds(off, WCOLS)] + d[s:s + 1, :] + vbo[:, pl.ds(off, WCOLS)])
+                for t in range(ctiles):
+                    xg[pl.ds(my_slot + p * XPR + s * XT + k * ctiles + t, 1), :] = v[:, t * LANES:(t + 1) * LANES]
             return 0
-        cp(me, ss.at[0], partner).start()
-        lax.fori_loop(1, chips, send, 0)
-
-        def fwd(i, _):
-            slot = peer(lax.rem(chip + chips - i, chips))
-            cp(slot, ss.at[0], partner).wait_recv()
-            cp(slot, fs.at[i], partner).start()
-            return 0
-        lax.fori_loop(1, chips, fwd, 0)
-
-        def other(i, _):
-            slot = lax.rem(chip + chips - i, chips) * CORES + (1 - c)
-            cp(slot, ss.at[0], partner).wait_recv()
-            return 0
-        lax.fori_loop(0, chips, other, 0)
-
-        def drain():
-            cp(me, ss.at[0], partner).wait_send()
-
-            def dr(i, _):
-                cp(me, ss.at[i], partner).wait_send()
-                cp(me, fs.at[i], partner).wait_send()
-                return 0
-            lax.fori_loop(1, chips, dr, 0)
-        return drain
-
-    x_drain = gather(xg, xa_s, xa_r, xf_s)
+        lax.fori_loop(0, 4 // XP, wo_other, 0)
+        x_send(p)
+    x_finish()
     for s in range(S):
         for hf in range(CORES):
             for t in range(HH):
-                x32[s * B:(s + 1) * B, (hf * HH + t) * LANES:(hf * HH + t + 1) * LANES] = xg[pl.ds(hf * QR + s * HH + t, B, stride=CORES * QR), :]
+                x32[s * B:(s + 1) * B, (hf * HH + t) * LANES:(hf * HH + t + 1) * LANES] = xg[pl.ds(hf * QR + (t // XT) * XPR + s * XT + t % XT, B, stride=CORES * QR), :]
 
     for s in range(S):
         layer_norm(s, vg2, vc2)
@@ -364,20 +436,19 @@
             idx = jnp.sum(jnp.where(diag, jnp.broadcast_to(ei_ref[s, k:k + 1, :], (B, B)).astype(F32), 0.0), axis=1, keepdims=True)
             gate = gate + jnp.where(le.astype(F32) == idx, p, 0.0)
         gs[s * B:(s + 1) * B, 0:E] = gate
-    g = gs[...]
-    step = E
-    while step < LANES:
-        g = g + pltpu.roll(g, step, 1)
-        step *= 2
+    gt[...] = jnp.transpose(gs[...])
+    g_e = jnp.concatenate([gt[0:E, :]] * (LANES // E), axis=0)[:, 0:R]
     moe_copies[0].wait()
     moe_copies[1].wait()
-    for t in range(FEP // 256):
-        ag = lax.dot_general(h[...], wmoe[0, t * 256:(t + 1) * 256, :], NT, preferred_element_type=F32)
-        au = lax.dot_general(h[...], wmoe[1, t * 256:(t + 1) * 256, :], NT, preferred_element_type=F32)
-        gg = jnp.concatenate([g] * (256 // LANES), axis=1)
+    UB = 256
+    for t in range(FEP // UB):
+        ag = lax.dot_general(wmoe[0, t * UB:(t + 1) * UB, :], h[...], NT, preferred_element_type=F32)
+        au = lax.dot_general(wmoe[1, t * UB:(t + 1) * UB, :], h[...], NT, preferred_element_type=F32)
+        gg = jnp.concatenate([g_e] * (UB // LANES), axis=0)
         u = gg * (ag * jax.nn.sigmoid(ag)) * au
-        u = jnp.where(iota((R, 256), 1) + t * 256 < FE, u, 0.0)
-        ub[:, t * 256:(t + 1) * 256] = u.astype(BF16)
+        ut[t * UB:(t + 1) * UB, 0:R] = jnp.where(iota((UB, R), 0) + t * UB < FE, u, 0.0)
+    for t in range(FEP // LANES):
+        ub[:, t * LANES:(t + 1) * LANES] = jnp.transpose(ut[t * LANES:(t + 1) * LANES, :])[0:R, :].astype(BF16)
     moe_copies[2].wait()
 
     def mo_copy(i):
@@ -389,20 +460,21 @@
         dst[di, :, :] = mine[i] + mprecv[i]
 
     def moe_step(j, _):
-        i = lax.rem(chip + 1 + j, chips)
+        i = nth(j)
         pp = round_bf16(jnp.dot(ub[...], wmoe[2, :, pl.ds(pl.multiple_of(i * PC, PC), PC)], preferred_element_type=F32))
         p0, p1 = pp[:, :LANES], pp[:, LANES:]
         mpsend[i, :, :] = jnp.where(c == 0, p1, p0)
         mine[i, :, :] = jnp.where(c == 0, p0, p1)
         to_partner(mpsend.at[i], mprecv.at[i], mp_s.at[i], mp_r.at[i]).start()
-
-        @pl.when(j > 0)
-        def _():
-            pi = lax.rem(chip + j, chips)
-            moe_pair(pi, mosend, pi)
-            mo_copy(pi).start()
         return 0
     lax.fori_loop(0, chips, moe_step, 0)
+
+    def moe_fwd(j, _):
+        i = nth(j)
+        moe_pair(i, mosend, i)
+        mo_copy(i).start()
+        return 0
+    lax.fori_loop(0, chips - 1, moe_fwd, 0)
     moe_pair(chip, morecv, chip)
 
     k_x.wait_recv()
@@ -424,7 +496,9 @@
     for i in range(1, chips):
         tot = tot + morecv[i]
     yg[pl.ds(my_slot, QR), :] = round_bf16(x32[:, pl.ds(pl.multiple_of(me * LANES, LANES), LANES)] + tot)
-    y_drain = gather(yg, ya_s, ya_r, yf_s)
+    y_send, y_finish, y_drain = gatherer(yg, 1, ya_s, ya_r, yf_s)
+    y_send(0)
+    y_finish()
     for d in range(chips * CORES):
         for s in range(S):
             out_ref[s, :, d * LANES:(d + 1) * LANES] = yg[d * QR + s * B:d * QR + (s + 1) * B, :].astype(BF16)
@@ -436,7 +510,7 @@
 
     def drain(i, _):
         b = lax.rem(chip + i, chips)
-        to_partner(psend.at[b], precv.at[b], ps_s.at[b], ps_r.at[b]).wait_send()
+        p_copy(b).wait_send()
         to_partner(mpsend.at[b], mprecv.at[b], mp_s.at[b], mp_r.at[b]).wait_send()
 
         @pl.when(i > 0)
@@ -447,6 +521,26 @@
     lax.fori_loop(0, chips, drain, 0)
     x_drain()
     y_drain()
+
+
+def copy_out(a, b, d, oa, ob, od, sem):
+    cps = [pltpu.make_async_copy(x, y, sem.at[i]) for i, (x, y) in enumerate(((a, oa), (b, ob), (d, od)))]
+    for cp in cps:
+        cp.start()
+    for cp in cps:
+        cp.wait()
+
+
+def finish(*arrs):
+    return pl.pallas_call(
+        copy_out,
+        name="copy_out",
+        out_shape=tuple(jax.ShapeDtypeStruct(a.shape, a.dtype) for a in arrs),
+        in_specs=[pl.BlockSpec(memory_space=pltpu.VMEM)] * len(arrs),
+        out_specs=(pl.BlockSpec(memory_space=pl.ANY),) * len(arrs),
+        scratch_shapes=[pltpu.SemaphoreType.DMA((len(arrs),))],
+        compiler_params=pltpu.CompilerParams(vmem_limit_bytes=1 << 20),
+    )(*arrs)
 
 
 def solution(mesh):
@@ -470,8 +564,8 @@
         dims = dict(S=S, B=B, D=D, T=T, KH=KH, HD=HD, H=H, E=E, FE=FE, chips=chips)
         half = HD // 2
         power = np.float32(ROPE_BASE) ** (np.arange(half, dtype=np.float32) * np.float32(2.0) / np.float32(HD))
-        pw = jnp.asarray(np.concatenate([power, power])[None, :].astype(np.float32))
-        lf = jnp.concatenate([long_factor, long_factor])[None, :]
+        pw = jnp.asarray(power[None, :].astype(np.float32))
+        lf = long_factor[None, :]
         row = lambda a: a.reshape(1, -1)
         args = (seq_len, expert_idx.transpose(0, 2, 1), route_mask,
                 x_first, next_emb, k_cache.reshape(B, T * KH, HD), v_cache.reshape(B, T * KH, HD), row(ln1_gain), row(ln1_bias),
@@ -480,17 +574,19 @@
         V = pltpu.VMEM
         DS = pltpu.SemaphoreType.DMA
         scratch = [
+            pltpu.SMEM((B,), jnp.int32), V(expert_idx.transpose(0, 2, 1).shape, jnp.int32), V(route_mask.shape, jnp.int32),
             V((4, D, WCOLS), BF16), V((B, T * KH, HD), BF16), V((B, T * KH, HD), BF16), V((3, FEP, D), BF16),
             V((S, B, D), BF16), V((R, D), F32), V((R, D), BF16),
             V((1, D), F32), V((1, D), F32), V((1, D), F32), V((1, D), F32), V((1, D), F32), V((1, w_q.shape[1]), F32),
-            V((1, w_k.shape[1]), F32), V((1, w_v.shape[1]), F32), V((1, HD), F32), V((1, HD), F32), V((E, D), BF16),
+            V((1, w_k.shape[1]), F32), V((1, w_v.shape[1]), F32), V((1, half), F32), V((1, half), F32), V((E, D), BF16),
             V((CORES, B * QR, HD), F32), V((R, HD), F32), V((R, HD), F32), V((CORES, KHH, R, HD), F32), V((CORES, KHH, R, HD), F32), V((2, 16, HD), F32),
-            V((B, MR, HD), F32), V((B, MR, HD), F32), V((B, MR, HD), F32), V((B, MR, HD), F32), V((chips + 1, MR, HD), F32),
-            V((CORES, QR, HD), F32), V((8, D), F32), V((n * QR, HD), F32), V((R, LANES), F32), V((R, FEP), BF16),
+            V((CORES * QR, LANES), F32), V((2, CORES * QR, T * KH), F32), V((2, CORES * QR, T * KH), BF16),
+            V((CORES, B, MR, HD), F32), V((B, MR, HD), F32), V((B, MR, HD), F32), V((chips + 1, MR, HD), F32),
+            V((CORES, QR, HD), F32), V((CORES, 8, HH * HD), F32), V((4, 8, WCOLS), F32), V((n * QR, HD), F32), V((LANES, LANES), F32), V((LANES, LANES), F32), V((FEP, LANES), F32), V((R, FEP), BF16),
             V((chips, R, LANES), F32), V((chips, R, LANES), F32), V((chips, R, LANES), F32), V((chips, R, LANES), F32), V((chips, R, LANES), F32),
             V((n * QR, LANES), F32), V((B * S * KH, HD), F32),
-            DS((10,)), DS((B,)), DS((B,)), DS((3,)), DS((13,)), DS, DS, DS, DS, DS, DS, DS((B,)), DS((B,)), DS((chips,)), DS((chips,)), DS, DS,
-            DS((chips,)), DS((n,)), DS((chips,)), DS((chips,)), DS((chips,)), DS((chips,)), DS((chips,)), DS((chips,)), DS((n,)), DS((chips,)),
+            DS((10,)), DS((B,)), DS((B,)), DS((3,)), DS((16,)), DS, DS, DS, DS, DS, DS, DS((B,)), DS((B,)), DS((chips,)), DS((chips,)), DS, DS,
+            DS((2, chips)), DS((2, n)), DS((2, chips)), DS((chips,)), DS((chips,)), DS((chips,)), DS((chips,)), DS((1, chips)), DS((1, n)), DS((1, chips)),
         ]
         vm = pl.BlockSpec(memory_space=pltpu.VMEM)
         anys = pl.BlockSpec(memory_space=pl.ANY)
@@ -498,11 +594,12 @@
             functools.partial(kernel, dims),
             name="decode_layer",
             out_shape=(jax.ShapeDtypeStruct((S, B, D), BF16), jax.ShapeDtypeStruct((B * S * KH, HD), BF16), jax.ShapeDtypeStruct((B * S * KH, HD), BF16)),
-            in_specs=[pl.BlockSpec(memory_space=pltpu.SMEM), vm, vm] + [anys] * (len(args) - 3),
+            in_specs=[anys] * len(args),
             out_specs=(vm, vm, vm),
             scratch_shapes=scratch,
             compiler_params=pltpu.CompilerParams(collective_id=0, has_side_effects=True, vmem_limit_bytes=VMEM_BYTES),
         )(*args)
+        hidden, tk, tv = finish(hidden, tk, tv)
         return hidden, tk.reshape(B, S, KH, HD), tv.reshape(B, S, KH, HD)
 
     replicated = P()

time: 90.2 us -> 72.6 us (0.80)
  Pallas kernels: 83.1 us -> 69 us
  local copies, waits for them, and re-layouts: 4.85 us -> 2.77 us
  other arithmetic: 1.32 us -> 0 us
    pallas_call x1, Pallas kernels: 83.1 us -> 68.2 us  [layer_steps(): pl.pallas_call(functools.partial(kernel, dims), name='decode_layer', out_...]
    unnamed x3 -> x6, local copies, waits for them, and re-layouts: 4.85 us -> 2.77 us
    broadcast_in_dim x1 -> x0, other arithmetic: 1.32 us -> none  [layer_steps(): lf = jnp.concatenate([long_factor, long_factor])[None, :]]
where the time goes in v3:
time: 72.6 us; the launch traced here: 72.4 us
  Pallas kernels  69 us (95%)
  local copies, waits for them, and re-layouts  2.77 us (4%)
    pallas_call x1, Pallas kernels, layer_steps(): pl.pallas_call(functools.partial(kernel, dims), name='decode_layer', out_...  68.2 us
    unnamed x6, local copies, waits for them, and re-layouts  2.77 us

profile of v3, /device:TPU:97, one launch (start us, length us, event | category | flops | bytes accessed | tf_op | source)
XLA Modules:
  0.0 72.4 jit_solution(2490276088686777482)
XLA Ops:
  0.6 68.2 %decode_layer.1 = (bf16[3,16,4096]{2,1,0:T(8,128)(2,1)}, bf16[384,128]{1,0:T(8,128)(2,1)}, bf16[384,128]{1,0:T(8,128)(2,1)}) custom-call(s32[16]{0:T(128)} %lens_h.1, s32[3,2,16]{2,1,0:T(2,128)} %bitcast.38, s32[3,16,2,16]{3,2,1,0:T(2,128)} %rm_h.1, bf16[16,4096]{1,0:T(8,128)(2,1)} %x_first.1, bf16[2,16,4096]{2,1,0:T(8,128)(2,1)} %next_emb.1, ...), custom_call_target="tpu_custom_call" | custom-call | tf_op jit(solution)/shard_map/decode_layer/pallas_call | solution.py:593
  68.8 0.0 copy-start
  68.8 1.0 %copy-done = bf16[3,16,4096]{2,1,0:T(8,128)(2,1)S(1)} copy-done((bf16[3,16,4096]{2,1,0:T(8,128)(2,1)S(1)}, bf16[3,16,4096]{2,1,0:T(8,128)(2,1)}, u32[]{:S(2)}) %copy-start) | copy-done | bytes 393240
  69.8 0.0 copy-start.1
  69.8 0.9 %copy-done.1 = bf16[384,128]{1,0:T(8,128)(2,1)S(1)} copy-done((bf16[384,128]{1,0:T(8,128)(2,1)S(1)}, bf16[384,128]{1,0:T(8,128)(2,1)}, u32[]{:S(2)}) %copy-start.1) | copy-done | bytes 98328
  70.7 0.0 copy-start.2
  70.7 0.9 %copy-done.2 = bf16[384,128]{1,0:T(8,128)(2,1)S(1)} copy-done((bf16[384,128]{1,0:T(8,128)(2,1)S(1)}, bf16[384,128]{1,0:T(8,128)(2,1)}, u32[]{:S(2)}) %copy-start.2) | copy-done | bytes 98328
  71.6 0.8 %copy_out.1 = (bf16[3,16,4096]{2,1,0:T(8,128)(2,1)}, bf16[384,128]{1,0:T(8,128)(2,1)}, bf16[384,128]{1,0:T(8,128)(2,1)}) custom-call(bf16[3,16,4096]{2,1,0:T(8,128)(2,1)S(1)} %copy-done, bf16[384,128]{1,0:T(8,128)(2,1)S(1)} %copy-done.1, bf16[384,128]{1,0:T(8,128)(2,1)S(1)} %copy-done.2), custom_call_target="tpu_custom_call" | custom-call | tf_op jit(solution)/shard_map/copy_out/pallas_call | solution.py:535
Async XLA Ops:
  68.8 1.0 %copy-start = (bf16[3,16,4096]{2,1,0:T(8,128)(2,1)S(1)}, bf16[3,16,4096]{2,1,0:T(8,128)(2,1)}, u32[]{:S(2)}) copy-start(bf16[3,16,4096]{2,1,0:T(8,128)(2,1)} %get-tuple-element.9.a) | copy-start | bytes 1179652
  69.8 0.9 %copy-start.1 = (bf16[384,128]{1,0:T(8,128)(2,1)S(1)}, bf16[384,128]{1,0:T(8,128)(2,1)}, u32[]{:S(2)}) copy-start(bf16[384,128]{1,0:T(8,128)(2,1)} %get-tuple-element.10.b) | copy-start | bytes 294916
  70.7 0.9 %copy-start.2 = (bf16[384,128]{1,0:T(8,128)(2,1)S(1)}, bf16[384,128]{1,0:T(8,128)(2,1)}, u32[]{:S(2)}) copy-start(bf16[384,128]{1,0:T(8,128)(2,1)} %get-tuple-element.11.d) | copy-start | bytes 294916

commit v4 on v3

--- a/solution.py
+++ b/solution.py
@@ -33,6 +33,12 @@
     return jnp.sum(jnp.where(pick, jnp.broadcast_to(col, (rows, LANES)), 0.0), axis=0, keepdims=True)
 
 
+def full_row(full):
+    rows = full.shape[0]
+    pick = iota((rows, LANES), 0) == iota((rows, LANES), 1)
+    return jnp.sum(jnp.where(pick, full, 0.0), axis=0, keepdims=True)
+
+
 def to_col(row, rows):
     pick = iota((rows, LANES), 0) == iota((rows, LANES), 1)
     return jnp.sum(jnp.where(pick, jnp.broadcast_to(row, (rows, LANES)), 0.0), axis=1, keepdims=True)
@@ -58,7 +64,7 @@
            x_first, next_emb, k_hbm, v_hbm, g1, c1, w_q, b_q, w_k, b_k, w_v, b_v, w_o, b_o, g2, c2, w_r, w_g, w_u, w_d, lf, pw,
            out_ref, tk_ref, tv_ref,
            lens_ref, ei_ref, rm_ref, wring, kbuf, vbuf, wmoe, xin, x32, h, vg1, vc1, vg2, vc2, vbo, vbq, vbk, vbv, vlf, vpw, vwr,
-           qbuf, cosb, sinb, kt, vt, tkv, kbias, sbuf, wbuf, part, precv, osend, orecv, oxs, lhs, wacc, xg, gs, gt, ut, ub, mine, mpsend, mprecv, mosend, morecv, yg, t32,
+           qbuf, cosb, sinb, kt, vt, tkv, kbias, sbuf, mbuf, wbuf, part, precv, osend, orecv, oxs, lhs, wacc, xg, gs, gt, ut, ub, mine, mpsend, mprecv, mosend, morecv, yg, t32,
            wsem, ksem, vsem, msem, ssem, qx_s, qx_r, kx_s, kx_r, vx_s, vx_r, ps_s, ps_r, os_s, os_r, ox_s, ox_r,
            xa_s, xa_r, xf_s, mp_s, mp_r, mo_s, mo_r, ya_s, ya_r, yf_s):
     S, B, D, T, KH, HD, H, E, FE, chips = (dims[k] for k in ("S", "B", "D", "T", "KH", "HD", "H", "E", "FE", "chips"))
@@ -172,6 +178,12 @@
     def rotate(x):
         return round_bf16(x * cosb[...] + pltpu.roll(x, HD // 2, 1) * sinb[...])
 
+    def kv_start(j, _):
+        b = nth(j)
+        kcopy(b).start()
+        vcopy(b).start()
+        return 0
+
     def q_chunk(ci, _):
         pltpu.make_async_copy(wsrc(0), wring.at[ci], wsem.at[ci]).wait()
         off = pl.multiple_of(c * half_cols + ci * WCOLS, WCOLS)
@@ -191,20 +203,13 @@
         def _():
             wcopy(5).start()
 
-            def kv_start(j, _):
-                b = nth(j)
-                kcopy(b).start()
-                vcopy(b).start()
-                return 0
-            lax.fori_loop(0, B, kv_start, 0)
-
         @pl.when(ci == 2)
         def _():
-            wcopy(6).start()
+            lax.fori_loop(0, B // 2, kv_start, 0)
 
         @pl.when(ci == 3)
         def _():
-            wcopy(7).start()
+            lax.fori_loop(B // 2, B, kv_start, 0)
         return 0
     lax.fori_loop(0, 4, q_chunk, 0)
 
@@ -220,14 +225,10 @@
     y = round_bf16(jnp.dot(h[...], wring[0], preferred_element_type=F32) + vbk[:, pl.ds(pl.multiple_of(c * WCOLS, WCOLS), WCOLS)])
     for t in range(KHH):
         kt[c, t, :, :] = rotate(y[:, t * HD:(t + 1) * HD])
-    wcopy(8).start()
     wcopy(5).wait()
     y = round_bf16(jnp.dot(h[...], wring[1], preferred_element_type=F32) + vbv[:, pl.ds(pl.multiple_of(c * WCOLS, WCOLS), WCOLS)])
     for t in range(KHH):
         vt[c, t, :, :] = y[:, t * HD:(t + 1) * HD]
-    wcopy(9).start()
-    for cp in moe_copies:
-        cp.start()
     k_x = to_partner(kt.at[c], kt.at[c], kx_s, kx_r)
     v_x = to_partner(vt.at[c], vt.at[c], vx_s, vx_r)
     k_x.start()
@@ -269,11 +270,12 @@
                 sbuf[u, :, lo:lo + LANES] = xx
                 mx = jnp.maximum(mx, xx)
         m = jnp.max(mx, axis=1, keepdims=True)
-        mu = jnp.where(lim > 0, m, 0.0)
-        return m, mu
-
-    def weigh(b, u, m, mu):
-        mub = jnp.broadcast_to(mu, (AR, LANES))
+        mbuf[u, :, :] = jnp.broadcast_to(m, (AR, LANES))
+
+    def weigh(b, u):
+        lim = lens_ref[b] - me * T
+        mb = mbuf[u]
+        mub = jnp.where(lim > 0, mb, 0.0)
         tot = jnp.zeros((AR, LANES), F32)
         for lo in range(0, NK, LANES):
             w = jnp.exp2((sbuf[u, :, lo:lo + LANES] - mub) * fac)
@@ -281,35 +283,50 @@
             wbuf[u, :, lo:lo + LANES] = w.astype(BF16)
         l = jnp.sum(tot, axis=1, keepdims=True)
         o = jnp.dot(wbuf[u], vbuf[b], preferred_element_type=F32)
-        ms = m * scale
+        ms = mb * scale
         for hf in range(CORES):
             part[hf, b, 0:QR, :] = o[hf * QR:(hf + 1) * QR, :]
-            part[hf, b, QR:MR, :] = stat_tile(to_row(ms[hf * QR:(hf + 1) * QR, :]), to_row(l[hf * QR:(hf + 1) * QR, :]))
-
-    def attn2(jj):
-        bs = [nth(jj * 2 + u) for u in range(2)]
-        for b in bs:
-            kcopy(b).wait()
-            vcopy(b).wait()
-        st = [scores(b, u) for u, b in enumerate(bs)]
-        for u, b in enumerate(bs):
-            weigh(b, u, *st[u])
-        for b in bs:
-            p_copy(b).start()
+            part[hf, b, QR:MR, :] = stat_tile(full_row(ms[hf * QR:(hf + 1) * QR, :]), to_row(l[hf * QR:(hf + 1) * QR, :]))
 
     def comb(b):
         pair_combine(b, osend, b)
         o_copy(b).start()
 
-    attn2(0)
-
-    def attn_step(jj, _):
-        attn2(jj)
-        comb(nth(jj * 2 - 2))
-        comb(nth(jj * 2 - 1))
-        return 0
-    lax.fori_loop(1, B // 2, attn_step, 0)
-    comb(nth(B - 2))
+    LAG = 3
+
+    def stage(j, u, last, lagged):
+        kb = nth(j)
+        vcopy(kb).wait()
+        if not last:
+            kcopy(nth(j + 1)).wait()
+            scores(nth(j + 1), 1 - u)
+        for k, at in enumerate((3, 6, 9, 12)):
+            @pl.when(j == at)
+            def _():
+                wcopy(6 + k).start()
+        if last:
+            for cp in moe_copies:
+                cp.start()
+        weigh(kb, u)
+        p_copy(kb).start()
+        if lagged:
+            comb(nth(j - LAG))
+
+    kcopy(nth(0)).wait()
+    scores(nth(0), 0)
+    for j in range(LAG):
+        stage(j, j % 2, False, False)
+
+    def attn_step(j, _):
+        for u in range(2):
+            @pl.when(lax.rem(j, 2) == u)
+            def _():
+                stage(j, u, False, True)
+        return 0
+    lax.fori_loop(LAG, B - 1, attn_step, 0)
+    stage(B - 1, (B - 1) % 2, True, True)
+    for j in range(B - LAG, B - 1):
+        comb(nth(j))
     pair_combine(chip, orecv, chip)
 
     for s in range(S):
@@ -421,6 +438,9 @@
             for t in range(HH):
                 x32[s * B:(s + 1) * B, (hf * HH + t) * LANES:(hf * HH + t + 1) * LANES] = xg[pl.ds(hf * QR + (t // XT) * XPR + s * XT + t % XT, B, stride=CORES * QR), :]
 
+    for cp in moe_copies:
+        cp.wait()
+
     for s in range(S):
         layer_norm(s, vg2, vc2)
     logits = lax.dot_general(h[...], vwr[...], NT, preferred_element_type=F32)
@@ -438,8 +458,6 @@
         gs[s * B:(s + 1) * B, 0:E] = gate
     gt[...] = jnp.transpose(gs[...])
     g_e = jnp.concatenate([gt[0:E, :]] * (LANES // E), axis=0)[:, 0:R]
-    moe_copies[0].wait()
-    moe_copies[1].wait()
     UB = 256
     for t in range(FEP // UB):
         ag = lax.dot_general(wmoe[0, t * UB:(t + 1) * UB, :], h[...], NT, preferred_element_type=F32)
@@ -449,7 +467,6 @@
         ut[t * UB:(t + 1) * UB, 0:R] = jnp.where(iota((UB, R), 0) + t * UB < FE, u, 0.0)
     for t in range(FEP // LANES):
         ub[:, t * LANES:(t + 1) * LANES] = jnp.transpose(ut[t * LANES:(t + 1) * LANES, :])[0:R, :].astype(BF16)
-    moe_copies[2].wait()
 
     def mo_copy(i):
         return pltpu.make_async_remote_copy(mosend.at[i], morecv.at[chip], mo_s.at[i], mo_r.at[chip],
@@ -459,22 +476,33 @@
         to_partner(mpsend.at[i], mprecv.at[i], mp_s.at[i], mp_r.at[i]).wait_recv()
         dst[di, :, :] = mine[i] + mprecv[i]
 
-    def moe_step(j, _):
-        i = nth(j)
-        pp = round_bf16(jnp.dot(ub[...], wmoe[2, :, pl.ds(pl.multiple_of(i * PC, PC), PC)], preferred_element_type=F32))
-        p0, p1 = pp[:, :LANES], pp[:, LANES:]
-        mpsend[i, :, :] = jnp.where(c == 0, p1, p0)
-        mine[i, :, :] = jnp.where(c == 0, p0, p1)
-        to_partner(mpsend.at[i], mprecv.at[i], mp_s.at[i], mp_r.at[i]).start()
-        return 0
-    lax.fori_loop(0, chips, moe_step, 0)
+    GRP = 4
+
+    def moe_out(g, _):
+        for k in range(GRP):
+            i = nth(g * GRP + k)
+            pp = round_bf16(jnp.dot(ub[...], wmoe[2, :, pl.ds(pl.multiple_of(i * PC, PC), PC)], preferred_element_type=F32))
+            p0, p1 = pp[:, :LANES], pp[:, LANES:]
+            mpsend[i, :, :] = jnp.where(c == 0, p1, p0)
+            mine[i, :, :] = jnp.where(c == 0, p0, p1)
+        for k in range(GRP):
+            i = nth(g * GRP + k)
+            to_partner(mpsend.at[i], mprecv.at[i], mp_s.at[i], mp_r.at[i]).start()
+        return 0
 
     def moe_fwd(j, _):
         i = nth(j)
         moe_pair(i, mosend, i)
         mo_copy(i).start()
         return 0
-    lax.fori_loop(0, chips - 1, moe_fwd, 0)
+    lax.fori_loop(0, 2, moe_out, 0)
+
+    def moe_both(g, _):
+        moe_out(g, 0)
+        lax.fori_loop((g - 2) * GRP, (g - 1) * GRP, moe_fwd, 0)
+        return 0
+    lax.fori_loop(2, chips // GRP, moe_both, 0)
+    lax.fori_loop(chips - 2 * GRP, chips - 1, moe_fwd, 0)
     moe_pair(chip, morecv, chip)
 
     k_x.wait_recv()
@@ -580,20 +608,20 @@
             V((1, D), F32), V((1, D), F32), V((1, D), F32), V((1, D), F32), V((1, D), F32), V((1, w_q.shape[1]), F32),
             V((1, w_k.shape[1]), F32), V((1, w_v.shape[1]), F32), V((1, half), F32), V((1, half), F32), V((E, D), BF16),
             V((CORES, B * QR, HD), F32), V((R, HD), F32), V((R, HD), F32), V((CORES, KHH, R, HD), F32), V((CORES, KHH, R, HD), F32), V((2, 16, HD), F32),
-            V((CORES * QR, LANES), F32), V((2, CORES * QR, T * KH), F32), V((2, CORES * QR, T * KH), BF16),
+            V((CORES * QR, LANES), F32), V((2, CORES * QR, T * KH), F32), V((2, CORES * QR, LANES), F32), V((2, CORES * QR, T * KH), BF16),
             V((CORES, B, MR, HD), F32), V((B, MR, HD), F32), V((B, MR, HD), F32), V((chips + 1, MR, HD), F32),
             V((CORES, QR, HD), F32), V((CORES, 8, HH * HD), F32), V((4, 8, WCOLS), F32), V((n * QR, HD), F32), V((LANES, LANES), F32), V((LANES, LANES), F32), V((FEP, LANES), F32), V((R, FEP), BF16),
             V((chips, R, LANES), F32), V((chips, R, LANES), F32), V((chips, R, LANES), F32), V((chips, R, LANES), F32), V((chips, R, LANES), F32),
             V((n * QR, LANES), F32), V((B * S * KH, HD), F32),
             DS((10,)), DS((B,)), DS((B,)), DS((3,)), DS((16,)), DS, DS, DS, DS, DS, DS, DS((B,)), DS((B,)), DS((chips,)), DS((chips,)), DS, DS,
-            DS((2, chips)), DS((2, n)), DS((2, chips)), DS((chips,)), DS((chips,)), DS((chips,)), DS((chips,)), DS((1, chips)), DS((1, n)), DS((1, chips)),
+            DS((2, chips)), DS((2, n)), DS((2, chips)), DS((chips,)), DS((chips,)), DS((chips,)), DS((chips,)), DS((2, chips)), DS((2, n)), DS((2, chips)),
         ]
         vm = pl.BlockSpec(memory_space=pltpu.VMEM)
         anys = pl.BlockSpec(memory_space=pl.ANY)
         hidden, tk, tv = pl.pallas_call(
             functools.partial(kernel, dims),
             name="decode_layer",
-            out_shape=(jax.ShapeDtypeStruct((S, B, D), BF16), jax.ShapeDtypeStruct((B * S * KH, HD), BF16), jax.ShapeDtypeStruct((B * S * KH, HD), BF16)),
+            out_shape=(V((S, B, D), BF16), V((B * S * KH, HD), BF16), V((B * S * KH, HD), BF16)),
             in_specs=[anys] * len(args),
             out_specs=(vm, vm, vm),
             scratch_shapes=scratch,

time: 72.6 us -> 67.8 us (0.934)
  local copies, waits for them, and re-layouts: 2.77 us -> 0 us
  Pallas kernels: 69 us -> 67.1 us
    unnamed x6 -> x0, local copies, waits for them, and re-layouts: 2.77 us -> none
    pallas_call x1, Pallas kernels: 68.2 us -> 66.3 us  [layer_steps(): pl.pallas_call(functools.partial(kernel, dims), name='decode_layer', out_...]
where the time goes in v4:
time: 67.8 us
  Pallas kernels  67.1 us (99%)
    pallas_call x1, Pallas kernels, layer_steps(): pl.pallas_call(functools.partial(kernel, dims), name='decode_layer', out_...  66.3 us

profile of v4, /device:TPU:97, one launch (start us, length us, event | category | flops | bytes accessed | tf_op | source)
XLA Modules:
  0.0 67.8 jit_solution(17350813371868926101)
XLA Ops:
  0.6 66.3 %decode_layer.1 = (bf16[3,16,4096]{2,1,0:T(8,128)(2,1)S(1)}, bf16[384,128]{1,0:T(8,128)(2,1)S(1)}, bf16[384,128]{1,0:T(8,128)(2,1)S(1)}) custom-call(s32[16]{0:T(128)} %lens_h.1, s32[3,2,16]{2,1,0:T(2,128)} %bitcast.38, s32[3,16,2,16]{3,2,1,0:T(2,128)} %rm_h.1, bf16[16,4096]{1,0:T(8,128)(2,1)} %x_first.1, bf16[2,16,4096]{2,1,0:T(8,128)(2,1)} %next_emb.1, ...), custom_call_target="tpu_custom_call" | custom-call | tf_op jit(solution)/shard_map/decode_layer/pallas_call | solution.py:621
  66.9 0.8 %copy_out.1 = (bf16[3,16,4096]{2,1,0:T(8,128)(2,1)}, bf16[384,128]{1,0:T(8,128)(2,1)}, bf16[384,128]{1,0:T(8,128)(2,1)}) custom-call(bf16[3,16,4096]{2,1,0:T(8,128)(2,1)S(1)} %get-tuple-element.9.a, bf16[384,128]{1,0:T(8,128)(2,1)S(1)} %get-tuple-element.10.b, bf16[384,128]{1,0:T(8,128)(2,1)S(1)} %get-tuple-element.11.d), custom_call_target="tpu_custom_call" | custom-call | tf_op jit(solution)/shard_map/copy_out/pallas_call | solution.py:563

commit v5 on v4

--- a/solution.py
+++ b/solution.py
@@ -64,9 +64,9 @@
            x_first, next_emb, k_hbm, v_hbm, g1, c1, w_q, b_q, w_k, b_k, w_v, b_v, w_o, b_o, g2, c2, w_r, w_g, w_u, w_d, lf, pw,
            out_ref, tk_ref, tv_ref,
            lens_ref, ei_ref, rm_ref, wring, kbuf, vbuf, wmoe, xin, x32, h, vg1, vc1, vg2, vc2, vbo, vbq, vbk, vbv, vlf, vpw, vwr,
-           qbuf, cosb, sinb, kt, vt, tkv, kbias, sbuf, mbuf, wbuf, part, precv, osend, orecv, oxs, lhs, wacc, xg, gs, gt, ut, ub, mine, mpsend, mprecv, mosend, morecv, yg, t32,
+           qbuf, cosb, sinb, kt, vt, tkv, kbias, sb0, sb1, mbuf, part, precv, osend, orecv, oxs, lhs, wacc, xg, gs, gt, ut, ub, mine, mpsend, mprecv, mosend, morecv, yg, t32,
            wsem, ksem, vsem, msem, ssem, qx_s, qx_r, kx_s, kx_r, vx_s, vx_r, ps_s, ps_r, os_s, os_r, ox_s, ox_r,
-           xa_s, xa_r, xf_s, mp_s, mp_r, mo_s, mo_r, ya_s, ya_r, yf_s):
+           xa_s, xa_r, xa_o, mp_s, mp_r, mo_s, mo_r, ya_s, ya_r, ya_o):
     S, B, D, T, KH, HD, H, E, FE, chips = (dims[k] for k in ("S", "B", "D", "T", "KH", "HD", "H", "E", "FE", "chips"))
     R = S * B
     HH, KHH = H // CORES, KH // CORES
@@ -236,6 +236,7 @@
 
     q_x.wait_recv()
     AR = CORES * QR
+    sbufs = (sb0, sb1)
     NK = T * KH
     fac = scale * math.log2(math.e)
     lane = iota((AR, LANES), 1)
@@ -256,37 +257,47 @@
         dst[di, 0:QR, :] = part[c, b, 0:QR, :] * to_col(f1, QR) + precv[b, 0:QR, :] * to_col(f2, QR)
         dst[di, QR:MR, :] = stat_tile(top, l1 * f1 + l2 * f2)
 
-    def scores(b, u):
-        lim = (lens_ref[b] - me * T) * KH
+    def queries(b):
         q0 = qbuf[0, pl.ds(pl.multiple_of(b * QR, QR), QR), :]
         q1 = qbuf[1, pl.ds(pl.multiple_of(b * QR, QR), QR), :]
-        qb = jnp.concatenate([q0, q1], axis=0).astype(BF16)
-        mx = jnp.full((AR, LANES), NEG_FILL, F32)
-        for col in range(NK // 256):
-            x = lax.dot_general(qb, kbuf[b, col * 256:(col + 1) * 256, :], NT, preferred_element_type=F32)
-            for hc in range(256 // LANES):
-                lo = col * 256 + hc * LANES
-                xx = jnp.where(lane < lim - lo, x[:, hc * LANES:(hc + 1) * LANES] + kbias[...], NEG_FILL)
-                sbuf[u, :, lo:lo + LANES] = xx
-                mx = jnp.maximum(mx, xx)
-        m = jnp.max(mx, axis=1, keepdims=True)
-        mbuf[u, :, :] = jnp.broadcast_to(m, (AR, LANES))
-
-    def weigh(b, u):
-        lim = lens_ref[b] - me * T
-        mb = mbuf[u]
-        mub = jnp.where(lim > 0, mb, 0.0)
-        tot = jnp.zeros((AR, LANES), F32)
-        for lo in range(0, NK, LANES):
-            w = jnp.exp2((sbuf[u, :, lo:lo + LANES] - mub) * fac)
-            tot = tot + w
-            wbuf[u, :, lo:lo + LANES] = w.astype(BF16)
-        l = jnp.sum(tot, axis=1, keepdims=True)
-        o = jnp.dot(wbuf[u], vbuf[b], preferred_element_type=F32)
-        ms = mb * scale
-        for hf in range(CORES):
-            part[hf, b, 0:QR, :] = o[hf * QR:(hf + 1) * QR, :]
-            part[hf, b, QR:MR, :] = stat_tile(full_row(ms[hf * QR:(hf + 1) * QR, :]), to_row(l[hf * QR:(hf + 1) * QR, :]))
+        return jnp.concatenate([q0, q1], axis=0).astype(BF16)
+
+    def work(sb, su, wb, wu):
+        CK = 256
+        if sb is not None:
+            lim = (lens_ref[sb] - me * T) * KH
+            qb = queries(sb)
+            mx = jnp.full((AR, LANES), NEG_FILL, F32)
+        if wb is not None:
+            mb = mbuf[wu]
+            mub = jnp.where(lens_ref[wb] > me * T, mb, 0.0)
+            tot = jnp.zeros((AR, LANES), F32)
+            o = jnp.zeros((AR, HD), F32)
+        for col in range(NK // CK):
+            if sb is not None:
+                x = lax.dot_general(qb, kbuf[sb, col * CK:(col + 1) * CK, :], NT, preferred_element_type=F32)
+            if wb is not None:
+                ws = []
+                for hc in range(CK // LANES):
+                    lo = col * CK + hc * LANES
+                    w = jnp.exp2((sbufs[wu][:, lo:lo + LANES] - mub) * fac)
+                    tot = tot + w
+                    ws.append(w.astype(BF16))
+                o = o + jnp.dot(jnp.concatenate(ws, axis=1), vbuf[wb, col * CK:(col + 1) * CK, :], preferred_element_type=F32)
+            if sb is not None:
+                for hc in range(CK // LANES):
+                    lo = col * CK + hc * LANES
+                    xx = jnp.where(lane < lim - lo, x[:, hc * LANES:(hc + 1) * LANES] + kbias[...], NEG_FILL)
+                    sbufs[su][:, lo:lo + LANES] = xx
+                    mx = jnp.maximum(mx, xx)
+        if sb is not None:
+            mbuf[su, :, :] = jnp.broadcast_to(jnp.max(mx, axis=1, keepdims=True), (AR, LANES))
+        if wb is not None:
+            l = jnp.sum(tot, axis=1, keepdims=True)
+            ms = mb * scale
+            for hf in range(CORES):
+                part[hf, wb, 0:QR, :] = o[hf * QR:(hf + 1) * QR, :]
+                part[hf, wb, QR:MR, :] = stat_tile(full_row(ms[hf * QR:(hf + 1) * QR, :]), to_row(l[hf * QR:(hf + 1) * QR, :]))
 
     def comb(b):
         pair_combine(b, osend, b)
@@ -299,7 +310,6 @@
         vcopy(kb).wait()
         if not last:
             kcopy(nth(j + 1)).wait()
-            scores(nth(j + 1), 1 - u)
         for k, at in enumerate((3, 6, 9, 12)):
             @pl.when(j == at)
             def _():
@@ -307,13 +317,13 @@
         if last:
             for cp in moe_copies:
                 cp.start()
-        weigh(kb, u)
+        work(None if last else nth(j + 1), 1 - u, kb, u)
         p_copy(kb).start()
         if lagged:
             comb(nth(j - LAG))
 
     kcopy(nth(0)).wait()
-    scores(nth(0), 0)
+    work(nth(0), 0, None, 0)
     for j in range(LAG):
         stage(j, j % 2, False, False)
 
@@ -385,41 +395,44 @@
     o_x.wait_recv()
     fill(1 - c)
 
-    def gatherer(buf, pieces, ss, rs, fs):
+    GROUPS = 3
+    GSIZE = -(-len(offsets) // GROUPS)
+
+    def gatherer(buf, pieces, ss, rs, ro):
         PR = QR // pieces
 
-        def cp(p, slot, sem, dev):
+        def cp(p, slot, rsem, dev):
             blk = buf.at[pl.ds(pl.multiple_of(slot * QR + p * PR, 8), PR)]
-            return pltpu.make_async_remote_copy(blk, blk, sem, rs.at[p, slot], device_id={"kv": dev}, device_id_type=MESH)
+            return pltpu.make_async_remote_copy(blk, blk, ss.at[p], rsem, device_id={"kv": dev}, device_id_type=MESH)
+
+        def all_of(count, p, rsem):
+            blk = buf.at[pl.ds(0, count * PR)]
+            return pltpu.make_async_remote_copy(blk, blk, ss.at[p], rsem, device_id={"kv": partner}, device_id_type=MESH)
 
         def send(p):
             for i, o in enumerate(offsets):
-                cp(p, me, ss.at[p, i], peer(ahead(o))).start()
-            cp(p, me, ss.at[p, len(offsets)], partner).start()
+                cp(p, me, rs.at[p, i // GSIZE], peer(ahead(o))).start()
+            cp(p, me, ro.at[p], partner).start()
 
         def finish():
             for p in range(pieces):
-                for i, o in enumerate(offsets):
-                    slot = peer(behind(o))
-                    cp(p, slot, ss.at[p, i], partner).wait_recv()
-                    cp(p, slot, fs.at[p, i], partner).start()
+                for g in range(GROUPS):
+                    mem = offsets[g * GSIZE:(g + 1) * GSIZE]
+                    all_of(len(mem), p, rs.at[p, g]).wait_recv()
+                    for o in mem:
+                        cp(p, peer(behind(o)), ro.at[p], partner).start()
             for p in range(pieces):
-                cp(p, partner, ss.at[p, 0], partner).wait_recv()
-                for i, o in enumerate(offsets):
-                    cp(p, behind(o) * CORES + (1 - c), ss.at[p, i], partner).wait_recv()
+                all_of(chips, p, ro.at[p]).wait_recv()
 
         def drain():
             for p in range(pieces):
-                cp(p, me, ss.at[p, len(offsets)], partner).wait_send()
-                for i in range(len(offsets)):
-                    cp(p, me, ss.at[p, i], partner).wait_send()
-                    cp(p, me, fs.at[p, i], partner).wait_send()
+                all_of(2 * chips - 1, p, ro.at[p]).wait_send()
         return send, finish, drain
 
     XP = 2
     XPR = QR // XP
     XT = HH // XP
-    x_send, x_finish, x_drain = gatherer(xg, XP, xa_s, xa_r, xf_s)
+    x_send, x_finish, x_drain = gatherer(xg, XP, xa_s, xa_r, xa_o)
     for p in range(XP):
         def wo_other(k, _):
             jn = p * (4 // XP) + k
@@ -468,13 +481,17 @@
     for t in range(FEP // LANES):
         ub[:, t * LANES:(t + 1) * LANES] = jnp.transpose(ut[t * LANES:(t + 1) * LANES, :])[0:R, :].astype(BF16)
 
-    def mo_copy(i):
-        return pltpu.make_async_remote_copy(mosend.at[i], morecv.at[chip], mo_s.at[i], mo_r.at[chip],
+    MP = 2
+    MPR = R // MP
+
+    def mo_copy(i, p):
+        return pltpu.make_async_remote_copy(mosend.at[p, i], morecv.at[p, chip], mo_s.at[p, i], mo_r.at[p, chip],
                                             device_id={"kv": peer(i)}, device_id_type=MESH)
 
     def moe_pair(i, dst, di):
         to_partner(mpsend.at[i], mprecv.at[i], mp_s.at[i], mp_r.at[i]).wait_recv()
-        dst[di, :, :] = mine[i] + mprecv[i]
+        for p in range(MP):
+            dst[p, di, :, :] = mine[i, p * MPR:(p + 1) * MPR, :] + mprecv[i, p * MPR:(p + 1) * MPR, :]
 
     GRP = 4
 
@@ -493,7 +510,7 @@
     def moe_fwd(j, _):
         i = nth(j)
         moe_pair(i, mosend, i)
-        mo_copy(i).start()
+        mo_copy(i, 0).start()
         return 0
     lax.fori_loop(0, 2, moe_out, 0)
 
@@ -503,6 +520,12 @@
         return 0
     lax.fori_loop(2, chips // GRP, moe_both, 0)
     lax.fori_loop(chips - 2 * GRP, chips - 1, moe_fwd, 0)
+
+    def mo_rest(j, _):
+        for p in range(1, MP):
+            mo_copy(nth(j), p).start()
+        return 0
+    lax.fori_loop(0, chips - 1, mo_rest, 0)
     moe_pair(chip, morecv, chip)
 
     k_x.wait_recv()
@@ -514,18 +537,19 @@
                     t32[pl.ds(s * KH + hf * KHH + t, B, stride=S * KH), :] = src[hf, t, s * B:(s + 1) * B, :]
         dst[...] = t32[...].astype(BF16)
 
-    def mo_wait(i, _):
-        src = lax.rem(chip + chips - i, chips)
-        pltpu.make_async_remote_copy(mosend.at[0], morecv.at[src], mo_s.at[0], mo_r.at[src],
-                                     device_id={"kv": peer(src)}, device_id_type=MESH).wait_recv()
-        return 0
-    lax.fori_loop(1, chips, mo_wait, 0)
-    tot = morecv[0]
-    for i in range(1, chips):
-        tot = tot + morecv[i]
-    yg[pl.ds(my_slot, QR), :] = round_bf16(x32[:, pl.ds(pl.multiple_of(me * LANES, LANES), LANES)] + tot)
-    y_send, y_finish, y_drain = gatherer(yg, 1, ya_s, ya_r, yf_s)
-    y_send(0)
+    y_send, y_finish, y_drain = gatherer(yg, MP, ya_s, ya_r, ya_o)
+    for p in range(MP):
+        def mo_wait(i, _):
+            src = lax.rem(chip + i, chips)
+            pltpu.make_async_remote_copy(mosend.at[p, 0], morecv.at[p, src], mo_s.at[p, 0], mo_r.at[p, src],
+                                         device_id={"kv": peer(src)}, device_id_type=MESH).wait_recv()
+            return 0
+        lax.fori_loop(1, chips, mo_wait, 0)
+        tot = morecv[p, 0]
+        for i in range(1, chips):
+            tot = tot + morecv[p, i]
+        yg[pl.ds(my_slot + p * MPR, MPR), :] = round_bf16(x32[p * MPR:(p + 1) * MPR, pl.ds(pl.multiple_of(me * LANES, LANES), LANES)] + tot)
+        y_send(p)
     y_finish()
     for d in range(chips * CORES):
         for s in range(S):
@@ -544,7 +568,8 @@
         @pl.when(i > 0)
         def _():
             o_copy(b).wait_send()
-            mo_copy(b).wait_send()
+            for p in range(MP):
+                mo_copy(b, p).wait_send()
         return 0
     lax.fori_loop(0, chips, drain, 0)
     x_drain()
@@ -608,13 +633,13 @@
             V((1, D), F32), V((1, D), F32), V((1, D), F32), V((1, D), F32), V((1, D), F32), V((1, w_q.shape[1]), F32),
             V((1, w_k.shape[1]), F32), V((1, w_v.shape[1]), F32), V((1, half), F32), V((1, half), F32), V((E, D), BF16),
             V((CORES, B * QR, HD), F32), V((R, HD), F32), V((R, HD), F32), V((CORES, KHH, R, HD), F32), V((CORES, KHH, R, HD), F32), V((2, 16, HD), F32),
-            V((CORES * QR, LANES), F32), V((2, CORES * QR, T * KH), F32), V((2, CORES * QR, LANES), F32), V((2, CORES * QR, T * KH), BF16),
+            V((CORES * QR, LANES), F32), V((CORES * QR, T * KH), F32), V((CORES * QR, T * KH), F32), V((2, CORES * QR, LANES), F32),
             V((CORES, B, MR, HD), F32), V((B, MR, HD), F32), V((B, MR, HD), F32), V((chips + 1, MR, HD), F32),
             V((CORES, QR, HD), F32), V((CORES, 8, HH * HD), F32), V((4, 8, WCOLS), F32), V((n * QR, HD), F32), V((LANES, LANES), F32), V((LANES, LANES), F32), V((FEP, LANES), F32), V((R, FEP), BF16),
-            V((chips, R, LANES), F32), V((chips, R, LANES), F32), V((chips, R, LANES), F32), V((chips, R, LANES), F32), V((chips, R, LANES), F32),
+            V((chips, R, LANES), F32), V((chips, R, LANES), F32), V((chips, R, LANES), F32), V((2, chips, R // 2, LANES), F32), V((2, chips, R // 2, LANES), F32),
             V((n * QR, LANES), F32), V((B * S * KH, HD), F32),
             DS((10,)), DS((B,)), DS((B,)), DS((3,)), DS((16,)), DS, DS, DS, DS, DS, DS, DS((B,)), DS((B,)), DS((chips,)), DS((chips,)), DS, DS,
-            DS((2, chips)), DS((2, n)), DS((2, chips)), DS((chips,)), DS((chips,)), DS((chips,)), DS((chips,)), DS((2, chips)), DS((2, n)), DS((2, chips)),
+            DS((2,)), DS((2, 3)), DS((2,)), DS((chips,)), DS((chips,)), DS((2, chips)), DS((2, chips)), DS((2,)), DS((2, 3)), DS((2,)),
         ]
         vm = pl.BlockSpec(memory_space=pltpu.VMEM)
         anys = pl.BlockSpec(memory_space=pl.ANY)

time: 67.8 us -> 63.8 us (0.941)
  Pallas kernels: 67.1 us -> 63 us
    pallas_call x1, Pallas kernels: 66.3 us -> 62.2 us  [layer_steps(): pl.pallas_call(functools.partial(kernel, dims), name='decode_layer', out_...]
where the time goes in v5:
time: 63.8 us; the launch traced here: 63.7 us
  Pallas kernels  63 us (99%)
  between operations  0.65 us (1%)
    pallas_call x1, Pallas kernels, layer_steps(): pl.pallas_call(functools.partial(kernel, dims), name='decode_layer', out_...  62.2 us

profile of v5, /device:TPU:97, one launch (start us, length us, event | category | flops | bytes accessed | tf_op | source)
XLA Modules:
  0.0 63.7 jit_solution(10014051235359459767)
XLA Ops:
  0.6 62.2 %decode_layer.1 = (bf16[3,16,4096]{2,1,0:T(8,128)(2,1)S(1)}, bf16[384,128]{1,0:T(8,128)(2,1)S(1)}, bf16[384,128]{1,0:T(8,128)(2,1)S(1)}) custom-call(s32[16]{0:T(128)} %lens_h.1, s32[3,2,16]{2,1,0:T(2,128)} %bitcast.38, s32[3,16,2,16]{3,2,1,0:T(2,128)} %rm_h.1, bf16[16,4096]{1,0:T(8,128)(2,1)} %x_first.1, bf16[2,16,4096]{2,1,0:T(8,128)(2,1)} %next_emb.1, ...), custom_call_target="tpu_custom_call" | custom-call | tf_op jit(solution)/shard_map/decode_layer/pallas_call | solution.py:646
  62.8 0.8 %copy_out.1 = (bf16[3,16,4096]{2,1,0:T(8,128)(2,1)}, bf16[384,128]{1,0:T(8,128)(2,1)}, bf16[384,128]{1,0:T(8,128)(2,1)}) custom-call(bf16[3,16,4096]{2,1,0:T(8,128)(2,1)S(1)} %get-tuple-element.9.a, bf16[384,128]{1,0:T(8,128)(2,1)S(1)} %get-tuple-element.10.b, bf16[384,128]{1,0:T(8,128)(2,1)S(1)} %get-tuple-element.11.d), custom_call_target="tpu_custom_call" | custom-call | tf_op jit(solution)/shard_map/copy_out/pallas_call | solution.py:588

commit v6 on v5

--- a/solution.py
+++ b/solution.py
@@ -66,7 +66,7 @@
            lens_ref, ei_ref, rm_ref, wring, kbuf, vbuf, wmoe, xin, x32, h, vg1, vc1, vg2, vc2, vbo, vbq, vbk, vbv, vlf, vpw, vwr,
            qbuf, cosb, sinb, kt, vt, tkv, kbias, sb0, sb1, mbuf, part, precv, osend, orecv, oxs, lhs, wacc, xg, gs, gt, ut, ub, mine, mpsend, mprecv, mosend, morecv, yg, t32,
            wsem, ksem, vsem, msem, ssem, qx_s, qx_r, kx_s, kx_r, vx_s, vx_r, ps_s, ps_r, os_s, os_r, ox_s, ox_r,
-           xa_s, xa_r, xa_o, mp_s, mp_r, mo_s, mo_r, ya_s, ya_r, ya_o):
+           xa_s, xa_r, xa_o, mo_s, mo_r, ya_s, ya_r, ya_o):
     S, B, D, T, KH, HD, H, E, FE, chips = (dims[k] for k in ("S", "B", "D", "T", "KH", "HD", "H", "E", "FE", "chips"))
     R = S * B
     HH, KHH = H // CORES, KH // CORES
@@ -78,7 +78,7 @@
     FEP = wmoe.shape[1]
     scale = HD ** -0.5
     me = lax.axis_index("kv")
-    chip = me // CORES
+    chip = lax.div(me, CORES)
     c = lax.rem(me, CORES)
     partner = chip * CORES + (1 - c)
 
@@ -86,13 +86,14 @@
         return ch * CORES + c
 
     side = math.isqrt(chips)
-    cy, cx = chip // side, lax.rem(chip, side)
+    cy, cx = lax.div(chip, side), lax.rem(chip, side)
 
     def ring(k):
-        return side // 2 + ((k + 1) // 2) * (1 - 2 * (k % 2))
+        return side // 2 + lax.div(k + 1, 2) * (1 - 2 * lax.rem(k, 2))
 
     def nth(j):
-        return lax.rem(cy + ring(j // side), side) * side + lax.rem(cx + ring(lax.rem(j, side)), side)
+        j = jnp.int32(j)
+        return lax.rem(cy + ring(lax.div(j, side)), side) * side + lax.rem(cx + ring(lax.rem(j, side)), side)
 
     def dist(d):
         return min(d, side - d)
@@ -303,7 +304,7 @@
         pair_combine(b, osend, b)
         o_copy(b).start()
 
-    LAG = 3
+    LAG = 2
 
     def stage(j, u, last, lagged):
         kb = nth(j)
@@ -445,6 +446,16 @@
             return 0
         lax.fori_loop(0, 4 // XP, wo_other, 0)
         x_send(p)
+
+    def o_drain(i, _):
+        b = lax.rem(chip + i, chips)
+        p_copy(b).wait_send()
+
+        @pl.when(i > 0)
+        def _():
+            o_copy(b).wait_send()
+        return 0
+    lax.fori_loop(0, chips, o_drain, 0)
     x_finish()
     for s in range(S):
         for hf in range(CORES):
@@ -489,7 +500,7 @@
                                             device_id={"kv": peer(i)}, device_id_type=MESH)
 
     def moe_pair(i, dst, di):
-        to_partner(mpsend.at[i], mprecv.at[i], mp_s.at[i], mp_r.at[i]).wait_recv()
+        to_partner(mpsend.at[i], mprecv.at[i], ps_s.at[i], ps_r.at[i]).wait_recv()
         for p in range(MP):
             dst[p, di, :, :] = mine[i, p * MPR:(p + 1) * MPR, :] + mprecv[i, p * MPR:(p + 1) * MPR, :]
 
@@ -504,7 +515,7 @@
             mine[i, :, :] = jnp.where(c == 0, p0, p1)
         for k in range(GRP):
             i = nth(g * GRP + k)
-            to_partner(mpsend.at[i], mprecv.at[i], mp_s.at[i], mp_r.at[i]).start()
+            to_partner(mpsend.at[i], mprecv.at[i], ps_s.at[i], ps_r.at[i]).start()
         return 0
 
     def moe_fwd(j, _):
@@ -562,12 +573,10 @@
 
     def drain(i, _):
         b = lax.rem(chip + i, chips)
-        p_copy(b).wait_send()
-        to_partner(mpsend.at[b], mprecv.at[b], mp_s.at[b], mp_r.at[b]).wait_send()
+        to_partner(mpsend.at[b], mprecv.at[b], ps_s.at[b], ps_r.at[b]).wait_send()
 
         @pl.when(i > 0)
         def _():
-            o_copy(b).wait_send()
             for p in range(MP):
                 mo_copy(b, p).wait_send()
         return 0
@@ -639,7 +648,7 @@
             V((chips, R, LANES), F32), V((chips, R, LANES), F32), V((chips, R, LANES), F32), V((2, chips, R // 2, LANES), F32), V((2, chips, R // 2, LANES), F32),
             V((n * QR, LANES), F32), V((B * S * KH, HD), F32),
             DS((10,)), DS((B,)), DS((B,)), DS((3,)), DS((16,)), DS, DS, DS, DS, DS, DS, DS((B,)), DS((B,)), DS((chips,)), DS((chips,)), DS, DS,
-            DS((2,)), DS((2, 3)), DS((2,)), DS((chips,)), DS((chips,)), DS((2, chips)), DS((2, chips)), DS((2,)), DS((2, 3)), DS((2,)),
+            DS((2,)), DS((2, 3)), DS((2,)), DS((2, chips)), DS((2, chips)), DS((2,)), DS((2, 3)), DS((2,)),
         ]
         vm = pl.BlockSpec(memory_space=pltpu.VMEM)
         anys = pl.BlockSpec(memory_space=pl.ANY)

time: 63.8 us -> 63.2 us (level)
  no operation moved by 1% of the time
where the time goes in v6:
time: 63.2 us; the launch traced here: 63.1 us
  Pallas kernels  62.4 us (99%)
  between operations  0.65 us (1%)
    pallas_call x1, Pallas kernels, layer_steps(): pl.pallas_call(functools.partial(kernel, dims), name='decode_layer', out_...  61.6 us

profile of v6, /device:TPU:97, one launch (start us, length us, event | category | flops | bytes accessed | tf_op | source)
XLA Modules:
  0.0 63.1 jit_solution(3881816369079422445)
XLA Ops:
  0.6 61.6 %decode_layer.1 = (bf16[3,16,4096]{2,1,0:T(8,128)(2,1)S(1)}, bf16[384,128]{1,0:T(8,128)(2,1)S(1)}, bf16[384,128]{1,0:T(8,128)(2,1)S(1)}) custom-call(s32[16]{0:T(128)} %lens_h.1, s32[3,2,16]{2,1,0:T(2,128)} %bitcast.38, s32[3,16,2,16]{3,2,1,0:T(2,128)} %rm_h.1, bf16[16,4096]{1,0:T(8,128)(2,1)} %x_first.1, bf16[2,16,4096]{2,1,0:T(8,128)(2,1)} %next_emb.1, ...), custom_call_target="tpu_custom_call" | custom-call | tf_op jit(solution)/shard_map/decode_layer/pallas_call | solution.py:655
  62.3 0.8 %copy_out.1 = (bf16[3,16,4096]{2,1,0:T(8,128)(2,1)}, bf16[384,128]{1,0:T(8,128)(2,1)}, bf16[384,128]{1,0:T(8,128)(2,1)}) custom-call(bf16[3,16,4096]{2,1,0:T(8,128)(2,1)S(1)} %get-tuple-element.9.a, bf16[384,128]{1,0:T(8,128)(2,1)S(1)} %get-tuple-element.10.b, bf16[384,128]{1,0:T(8,128)(2,1)S(1)} %get-tuple-element.11.d), custom_call_target="tpu_custom_call" | custom-call | tf_op jit(solution)/shard_map/copy_out/pallas_call | solution.py:597

commit v7 on v6

--- a/solution.py
+++ b/solution.py
@@ -174,7 +174,7 @@
     sinb[:, 0:hd2] = -sn
     sinb[:, hd2:HD] = sn
     kr, kl = iota((CORES * QR, LANES), 0), iota((CORES * QR, LANES), 1)
-    kbias[...] = jnp.where((kr // QR) * KHH + lax.rem(kr, HH) // QG == lax.rem(kl, KH), 0.0, NEG_FILL)
+    kbias[...] = jnp.where((kr // QR) * KHH + lax.rem(kr, HH) // QG == lax.rem(kl, KH), float(jnp.finfo(F32).max), NEG_FILL)
 
     def rotate(x):
         return round_bf16(x * cosb[...] + pltpu.roll(x, HD // 2, 1) * sinb[...])
@@ -288,7 +288,7 @@
             if sb is not None:
                 for hc in range(CK // LANES):
                     lo = col * CK + hc * LANES
-                    xx = jnp.where(lane < lim - lo, x[:, hc * LANES:(hc + 1) * LANES] + kbias[...], NEG_FILL)
+                    xx = jnp.where(lane < lim - lo, jnp.minimum(x[:, hc * LANES:(hc + 1) * LANES], kbias[...]), NEG_FILL)
                     sbufs[su][:, lo:lo + LANES] = xx
                     mx = jnp.maximum(mx, xx)
         if sb is not None:

time: 63.2 us -> 63.2 us (level)
  no operation moved by 1% of the time
where the time goes in v7:
time: 63.2 us; the launch traced here: 63.1 us
  Pallas kernels  62.5 us (99%)
  between operations  0.65 us (1%)
    pallas_call x1, Pallas kernels, layer_steps(): pl.pallas_call(functools.partial(kernel, dims), name='decode_layer', out_...  61.6 us

profile of v7, /device:TPU:97, one launch (start us, length us, event | category | flops | bytes accessed | tf_op | source)
XLA Modules:
  0.0 63.1 jit_solution(10960351471065512310)
XLA Ops:
  0.6 61.6 %decode_layer.1 = (bf16[3,16,4096]{2,1,0:T(8,128)(2,1)S(1)}, bf16[384,128]{1,0:T(8,128)(2,1)S(1)}, bf16[384,128]{1,0:T(8,128)(2,1)S(1)}) custom-call(s32[16]{0:T(128)} %lens_h.1, s32[3,2,16]{2,1,0:T(2,128)} %bitcast.38, s32[3,16,2,16]{3,2,1,0:T(2,128)} %rm_h.1, bf16[16,4096]{1,0:T(8,128)(2,1)} %x_first.1, bf16[2,16,4096]{2,1,0:T(8,128)(2,1)} %next_emb.1, ...), custom_call_target="tpu_custom_call" | custom-call | tf_op jit(solution)/shard_map/decode_layer/pallas_call | solution.py:655
  62.3 0.8 %copy_out.1 = (bf16[3,16,4096]{2,1,0:T(8,128)(2,1)}, bf16[384,128]{1,0:T(8,128)(2,1)}, bf16[384,128]{1,0:T(8,128)(2,1)}) custom-call(bf16[3,16,4096]{2,1,0:T(8,128)(2,1)S(1)} %get-tuple-element.9.a, bf16[384,128]{1,0:T(8,128)(2,1)S(1)} %get-tuple-element.10.b, bf16[384,128]{1,0:T(8,128)(2,1)S(1)} %get-tuple-element.11.d), custom_call_target="tpu_custom_call" | custom-call | tf_op jit(solution)/shard_map/copy_out/pallas_call | solution.py:597
